TPU v7x, 32 devices: a whole 2x2x4 slice. The times are simulated.
32 devices in a mesh: grp: 4 (over x, core), dev: 8 (over z, y).
Axes of the slice: x: 2, y: 2, z: 4, core: 2. Of those that a mesh axis runs over, the one named last changes fastest.
Arguments:
- density: bfloat16 [12288, 12288], P('grp', 'dev'), may hold values from -0.0546875 to 0.0546875
- left_factor: bfloat16 [512, 12288], P('dev', 'grp'), may hold values from -3 to 3
- right_factor: bfloat16 [512, 12288], P(None, 'dev'), may hold values from -3 to 3
- directions: float32 [3, 12288], P(None, 'dev'), may hold values from -1 to 1
- places: float32 [3, 4, 8, 4096], P(None, 'grp', 'dev'), may hold values from 0 to 8, as said below
- alpha: float32 [4, 8, 4096], P('grp', 'dev'), may hold values from 0.4 to 1.6
- static_field: float32 [3, 4, 8, 4096], P(None, 'grp', 'dev'), may hold values from -6 to 6
- neighbours: int32 [4, 8, 32, 12], P('grp', 'dev'), may hold values from 0 to 287, as said below
- targets: int32 [4, 8, 16], P('grp', 'dev'), may hold values from 0 to 4095, as said below
Outputs:
- dipoles: float32 [3, 4, 8, 4096], P(None, 'grp', 'dev')
- qm_field: float32 [3, 512], P(None, ('grp', 'dev'))
- fock_polar: float32 [12288, 12288], P('grp', 'dev')
Inputs may be any that keep to these rules, and one draw needn't show every extreme that they name: `places`: site s of brick (g, d) lies at x in [0.1 g, 0.1 (g + 1)), y in [0.1 d, 0.1 (d + 1)), z in [0.03 k, 0.03 (k + 1)) with k = s // 128. `neighbours`: entries of one row differ; the first names the block itself (brick part 4, the centre of the 3 x 3 bricks, i.e. 4 * 32 + b); every entry names a block of the 3 x 3 bricks around the own brick whose index along the third coordinate is within 2 of the block's own and inside 0 to 31. The targets of one brick are distinct sites.
All inputs are finite; a program needn't handle non-finite values.
Results may differ from a plain program's by a relative error of at most 0.0029.
Values may be sent and summed in bfloat16 or wider, within the bound.
No kernel may reach another device: no remote copies, remote signals or barrier semaphores. Data moves between devices by JAX's collectives and lax.ppermute only.
A program may use at most 128 MiB of HBM per device.

v0:
```python
import jax
import jax.numpy as jnp
from jax import lax
from jax.sharding import PartitionSpec as P

SWEEPS = 4


coupling = 2e-07
soften = 4e-05
blocks_per_turn = 4


def padded(block, sides, width):
    for axis, dim in sides:
        count = lax.axis_size(axis)
        forward = [(i, i + 1) for i in range(count - 1)]
        backward = [(target, source) for source, target in forward]
        low = lax.ppermute(
            lax.slice_in_dim(block, block.shape[dim] - width, None, axis=dim), axis, forward
        )
        high = lax.ppermute(lax.slice_in_dim(block, 0, width, axis=dim), axis, backward)
        block = jnp.concatenate([low, block, high], axis=dim)
    return block


def pair_field(own_sites, region_places, region_dipoles, links):
    blocks, listed = links.shape
    width = region_places.shape[2]
    turns = blocks // blocks_per_turn
    own_groups = own_sites.reshape(3, turns, blocks_per_turn, width).transpose(1, 0, 2, 3)
    link_groups = links.reshape(turns, blocks_per_turn, listed)
    column = jnp.arange(listed * width, dtype=jnp.int32)[None, :]
    row_ids = jnp.arange(width, dtype=jnp.int32)[:, None]
    keeper = column != row_ids

    def one_group(pieces):
        own_group, link_group = pieces
        near_places = region_places[:, link_group].reshape(3, blocks_per_turn, listed * width)
        near_dipoles = region_dipoles[:, link_group].reshape(3, blocks_per_turn, listed * width)
        offsets = own_group[:, :, :, None] - near_places[:, :, None, :]
        square = jnp.sum(offsets * offsets, axis=0) + soften
        inverse_cube = jnp.where(keeper, lax.rsqrt(square) / square, jnp.zeros_like(square))
        inverse_fifth = inverse_cube / square
        projection = jnp.sum(offsets * near_dipoles[:, :, None, :], axis=0)
        first_part = 3.0 * jnp.sum(offsets * (projection * inverse_fifth)[None], axis=-1)
        second_part = jnp.sum(near_dipoles[:, :, None, :] * inverse_cube[None], axis=-1)
        return coupling * (first_part - second_part)

    fields = lax.map(one_group, (own_groups, link_groups))
    return fields.transpose(1, 0, 2, 3).reshape(3, blocks * width)


def on_device(
    density, left_factor, right_factor, directions, places, alpha, static_field, neighbours, targets
):
    gathered = lax.all_gather(left_factor, "dev", axis=0, tiled=True)
    context = jnp.dot(gathered, density, preferred_element_type=jnp.float32)
    weighted = context * right_factor.astype(jnp.float32)
    partial_field = jnp.einsum("tn,kn->kt", weighted, directions, precision=lax.Precision.HIGHEST)
    per_brick = targets.shape[2]
    site_count = places.shape[3]
    groups = lax.axis_size("grp")
    members = lax.axis_size("dev")
    stacked = partial_field.reshape(3, groups, members, per_brick)
    within = lax.psum_scatter(stacked, "dev", scatter_dimension=2, tiled=True)
    qm_local = lax.psum_scatter(within, "grp", scatter_dimension=1, tiled=True).reshape(
        3, per_brick
    )
    picks = (targets[0, 0][:, None] == jnp.arange(site_count, dtype=jnp.int32)[None, :]).astype(
        jnp.float32
    )
    total = static_field[:, 0, 0] + jnp.dot(qm_local, picks, precision=lax.Precision.HIGHEST)
    polar = alpha[0, 0][None, :]
    own_sites = places[:, 0, 0]
    links = neighbours[0, 0]
    blocks = links.shape[0]
    width = site_count // blocks
    region_places = padded(places, (("grp", 1), ("dev", 2)), 1).reshape(3, 9 * blocks, width)
    current = polar * total
    for repeat in range(SWEEPS):
        region_dipoles = padded(current[:, None, None, :], (("grp", 1), ("dev", 2)), 1).reshape(
            3, 9 * blocks, width
        )
        current = polar * (total + pair_field(own_sites, region_places, region_dipoles, links))
    local_targets = jnp.dot(current, picks.T, precision=lax.Precision.HIGHEST)
    all_targets = lax.all_gather(local_targets, ("grp", "dev"), axis=1, tiled=True)
    along = jnp.einsum("kt,kn->tn", all_targets, directions, precision=lax.Precision.HIGHEST)
    scaled = (right_factor.astype(jnp.float32) * along).astype(jnp.bfloat16)
    contract = (((0,), (0,)), ((), ()))
    fock_polar = -lax.dot_general(gathered, scaled, contract, preferred_element_type=jnp.float32)
    return (current[:, None, None, :], qm_local, fock_polar)


def solution(mesh):
    placed = (
        P("grp", "dev"),
        P("dev", "grp"),
        P(None, "dev"),
        P(None, "dev"),
        P(None, "grp", "dev", None),
        P("grp", "dev", None),
        P(None, "grp", "dev", None),
        P("grp", "dev", None, None),
        P("grp", "dev", None),
    )
    return jax.shard_map(
        on_device,
        mesh=mesh,
        in_specs=placed,
        out_specs=(P(None, "grp", "dev", None), P(None, ("grp", "dev")), P("grp", "dev")),
        check_vma=False,
    )
```

profile of v0, /device:TPU:0, one launch (start us, length us, event | category | flops | bytes accessed | tf_op | source)
XLA Modules:
  0.0 550.1 jit_solution(6868844074491338189)
XLA Ops:
  16.5 56.4 %all-gather.3.cloned.1.call-done = bf16[512,3072]{1,0:T(8,128)(2,1)} async-done(((bf16[64,3072]{1,0:T(8,128)(2,1)}), bf16[512,3072]{1,0:T(8,128)(2,1)}) %all-gather.3.cloned.1.call-update) | async-done | bytes 3145744 | tf_op jit(solution)/shard_map/all_gather | solution.py:57
  72.9 9.6 %convert_multiply_fusion.1 = f32[512,1536]{1,0:T(8,128)S(1)} fusion(bf16[512,1536]{1,0:T(8,128)(2,1)} %param.19, bf16[512,3072]{1,0:T(8,128)(2,1)} %all-gather.3.cloned.1.call-done, bf16[3072,1536]{1,0:T(8,128)(2,1)} %param.17), kind=kOutput, calls=%fused_computation.83 | convolution fusion | flops 4833411072 | bytes 17301504 | tf_op jit(solution)/shard_map/dot_general | solution.py:58
  82.6 2.8 convolution_bitcast_fusion
  85.5 35.3 %all-reduce = f32[3,4,8,16]{3,1,0,2:T(4,128)S(1)} all-reduce(f32[3,4,8,16]{3,1,0,2:T(4,128)S(1)} %copy.124), channel_id=2, replica_groups=mesh['grp'=4,'dev'=8] {'dev'}, use_global_device_ids=true, to_apply=%region_0.0.clone | all-reduce | flops 1536 | bytes 12288
  121.5 5.8 %all-reduce.1 = f32[3,4,1,16]{3,2,0,1:T(1,128)S(1)} all-reduce(f32[3,4,1,16]{3,2,0,1:T(1,128)S(1)} %copy.125), channel_id=3, replica_groups=mesh['grp'=4,'dev'=8] {'grp'}, use_global_device_ids=true, to_apply=%region_1.0.clone | all-reduce | flops 192 | bytes 1536
  129.6 3.0 collective-permute-start.4
  134.0 4.6 collective-permute-start.2
  139.9 4.6 collective-permute-start.6
  148.1 2.9 collective-permute-done.6
  151.2 58.3 %while.44 = (s32[]{:T(128)}, f32[8,3,4,128]{3,2,1,0:T(4,128)S(1)}, f32[8,3,4,128]{3,2,1,0:T(4,128)S(1)}, s32[8,4,12]{2,1,0:T(4,128)S(1)}, f32[3,288,128]{2,0,1:T...) while((s32[]{:T(128)}, f32[8,3,4,128]{3,2,1,0:T(4,128)S(1)}, f32[8,3,4,128]{3,2,1,0:T(4,128)S(1)}, ...), condition=%wide.region_7.8_spmd.clone, body=%wide.region_2.7_spmd.clone.sunk | while | flops 26151568 | bytes 26799520 | solution.py:50
  152.8 2.7 fusion.45
  160.1 2.7 fusion.45
  167.4 2.7 fusion.45
  174.7 2.7 fusion.45
  182.0 2.7 fusion.45
  189.2 2.7 fusion.45
  203.8 2.7 fusion.45
  211.0 3.0 collective-permute-start.8
  216.2 5.2 collective-permute-start.10
  224.0 5.7 %collective-permute-done.10 = f32[3,3,1,4096]{3,0,2,1:T(4,128)S(1)} collective-permute-done((f32[3,3,1,4096]{3,0,2,1:T(4,128)S(1)}, f32[3,3,1,4096]{3,0,2,1:T(4,128)S(1)}, u32[]{:S(2)}, u32[]{:S(2)}) %collective-permute-start.10) | collective-permute-done | bytes 147488 | tf_op jit(solution)/shard_map/ppermute | solution.py:19
  229.8 58.3 %while.45 = (s32[]{:T(128)}, f32[8,3,4,128]{3,2,1,0:T(4,128)S(1)}, f32[8,3,4,128]{3,2,1,0:T(4,128)S(1)}, s32[8,4,12]{2,1,0:T(4,128)S(1)}, f32[3,288,128]{2,0,1:T...) while((s32[]{:T(128)}, f32[8,3,4,128]{3,2,1,0:T(4,128)S(1)}, ...), condition=%wide.region_13.14_spmd.clone, body=%wide.region_8.13_spmd.clone.sunk | while | flops 26151568 | bytes 26799520 | solution.py:50
  231.4 2.7 fusion.47
  246.0 2.7 fusion.47
  267.8 2.7 fusion.47
  275.1 2.7 fusion.47
  282.4 2.7 fusion.47
  289.6 3.0 collective-permute-start.12
  294.8 5.0 collective-permute-start.14
  302.6 5.7 %collective-permute-done.14 = f32[3,3,1,4096]{3,0,2,1:T(4,128)S(1)} collective-permute-done((f32[3,3,1,4096]{3,0,2,1:T(4,128)S(1)}, f32[3,3,1,4096]{3,0,2,1:T(4,128)S(1)}, u32[]{:S(2)}, u32[]{:S(2)}) %collective-permute-start.14) | collective-permute-done | bytes 147488 | tf_op jit(solution)/shard_map/ppermute | solution.py:19
  308.4 58.3 %while.46 = (s32[]{:T(128)}, f32[8,3,4,128]{3,2,1,0:T(4,128)S(1)}, f32[8,3,4,128]{3,2,1,0:T(4,128)S(1)}, s32[8,4,12]{2,1,0:T(4,128)S(1)}, f32[3,288,128]{2,0,1:T...) while((s32[]{:T(128)}, f32[8,3,4,128]{3,2,1,0:T(4,128)S(1)}, ...), condition=%wide.region_19.20_spmd.clone, body=%wide.region_14.19_spmd.clone.sunk | while | flops 26151568 | bytes 26799520 | solution.py:50
  310.0 2.7 fusion.49
  317.3 2.7 fusion.49
  331.9 2.7 fusion.49
  339.1 2.7 fusion.49
  346.4 2.7 fusion.49
  353.7 2.7 fusion.49
  361.0 2.7 fusion.49
  368.1 3.0 collective-permute-start.16
  373.4 5.2 collective-permute-start.18
  381.2 5.7 %collective-permute-done.18 = f32[3,3,1,4096]{3,0,2,1:T(4,128)S(1)} collective-permute-done((f32[3,3,1,4096]{3,0,2,1:T(4,128)S(1)}, f32[3,3,1,4096]{3,0,2,1:T(4,128)S(1)}, u32[]{:S(2)}, u32[]{:S(2)}) %collective-permute-start.18) | collective-permute-done | bytes 147488 | tf_op jit(solution)/shard_map/ppermute | solution.py:19
  387.0 58.3 %while.47 = (s32[]{:T(128)}, f32[8,3,4,128]{3,2,1,0:T(4,128)S(1)}, f32[8,3,4,128]{3,2,1,0:T(4,128)S(1)}, s32[8,4,12]{2,1,0:T(4,128)S(1)}, f32[3,288,128]{2,0,1:T...) while((s32[]{:T(128)}, f32[8,3,4,128]{3,2,1,0:T(4,128)S(1)}, ...), condition=%wide.region_25.26_spmd.clone, body=%wide.region_20.25_spmd.clone.sunk | while | flops 26151568 | bytes 26799520 | solution.py:50
  388.6 2.7 fusion.51
  395.9 2.7 fusion.51
  403.2 2.7 fusion.51
  446.5 66.1 %all-gather = f32[32,16,3]{1,2,0:T(4,128)S(1)} all-gather(f32[1,16,3]{1,2,0:T(4,128)S(1)} %convolution_bitcast_fusion.1), channel_id=1, replica_groups=mesh['grp'=4,'dev'=8] {'grp','dev'}, dimensions={0}, use_global_device_ids=true | all-gather | bytes 6336 | tf_op jit(solution)/shard_map/all_gather | solution.py:87
  512.7 2.8 fusion.24
  515.5 9.1 %negate_bitcast_fusion = f32[3072,1536]{0,1:T(8,128)} fusion(bf16[512,1536]{1,0:T(8,128)(2,1)S(1)} %fusion.24, bf16[512,3072]{1,0:T(8,128)(2,1)S(1)} %copy-done.4), kind=kOutput, calls=%fused_computation.80 | convolution fusion | flops 4836556800 | bytes 23592960 | tf_op jit(solution)/shard_map/dot_general | solution.py:91
  524.6 18.6 %copy.149 = f32[3072,1536]{1,0:T(8,128)} copy(f32[3072,1536]{0,1:T(8,128)} %negate_bitcast_fusion) | data formatting | bytes 37748736
  (549 shorter events, 208.9 us)
Async XLA Ops:
  7.2 75.4 %copy-start = (f32[3,1536]{1,0:T(4,128)S(1)}, f32[3,1536]{1,0:T(4,128)}, u32[]{:S(2)}) copy-start(f32[3,1536]{1,0:T(4,128)} %param.20) | copy-start | bytes 55300
  7.2 65.8 %all-gather.3.cloned.1.call-start = ((), (), s32[]{:S(2)}) async-start(), calls=%async_computation | async-start | bytes 3538944 | tf_op jit(solution)/shard_map/all_gather | solution.py:57
  7.9 7.8 %collective-permute-start = (f32[3,1,1,4096]{3,2,1,0:T(1,128)}, f32[3,1,1,4096]{3,2,1,0:T(1,128)S(1)}, u32[]{:S(2)}, u32[]{:S(2)}) collective-permute-start(f32[3,1,1,4096]{3,2,1,0:T(1,128)} %param.21), channel_id=1, source_target_pairs={{0,8},{8,16},{16,24},{1,9},{9,17},{17,25},{2,10},{10,18},{18,26},{... | collective-permute-start | bytes 147464 | tf_op jit(solution)/shard_map/ppermute | solution.py:19
  10.3 122.3 %collective-permute-start.1 = (f32[3,1,1,4096]{3,2,1,0:T(1,128)}, f32[3,1,1,4096]{3,2,1,0:T(1,128)S(1)}, u32[]{:S(2)}, u32[]{:S(2)}) collective-permute-start(f32[3,1,1,4096]{3,2,1,0:T(1,128)} %param.21), channel_id=1, source_target_pairs={{8,0},{16,8},{24,16},{9,1},{17,9},{25,17},{10,2},{18,10},{26,18},{... | collective-permute-start | bytes 147464 | tf_op jit(solution)/shard_map/ppermute | solution.py:22
  82.6 45.4 %copy-start.5 = (f32[3,1,1,4096]{3,2,1,0:T(1,128)S(1)}, f32[3,1,1,4096]{3,2,1,0:T(1,128)}, u32[]{:S(2)}) copy-start(f32[3,1,1,4096]{3,2,1,0:T(1,128)} %param.23) | copy-start | bytes 147460
  82.6 45.4 %copy-start.6 = (s32[1,1,16]{2,1,0:T(1,128)S(1)}, s32[1,1,16]{2,1,0:T(1,128)}, u32[]{:S(2)}) copy-start(s32[1,1,16]{2,1,0:T(1,128)} %param.25) | copy-start | bytes 196
  82.6 45.6 %copy-start.2 = (f32[1,1,4096]{2,1,0:T(1,128)S(1)}, f32[1,1,4096]{2,1,0:T(1,128)}, u32[]{:S(2)}) copy-start(f32[1,1,4096]{2,1,0:T(1,128)} %param.22) | copy-start | bytes 49156
  128.0 16.5 %copy-start.3 = (f32[3,1,1,16]{3,0,2,1:T(4,128)}, f32[3,1,1,16]{3,0,2,1:T(4,128)S(1)}, u32[]{:S(2)}) copy-start(f32[3,1,1,16]{3,0,2,1:T(4,128)S(1)} %copy.178) | copy-start | bytes 580
  128.3 10.2 %collective-permute-start.5 = (f32[3,1,1,4096]{3,0,2,1:T(4,128)S(1)}, f32[3,1,1,4096]{3,0,2,1:T(4,128)S(1)}, u32[]{:S(2)}, u32[]{:S(2)}) collective-permute-start(f32[3,1,1,4096]{3,0,2,1:T(4,128)S(1)} %multiply_bitcast_fusion.3), channel_id=1, source_target_pairs={{8,0},{16,8},{24,16},{9,1},{17,9},{25,17},{10,2},{18,10},{26,18},{... | collective-permute-start | bytes 147464 | tf_op jit(solution)/shard_map/ppermute | solution.py:22
  129.6 8.9 %collective-permute-start.4 = (f32[3,1,1,4096]{3,0,2,1:T(4,128)S(1)}, f32[3,1,1,4096]{3,0,2,1:T(4,128)S(1)}, u32[]{:S(2)}, u32[]{:S(2)}) collective-permute-start(f32[3,1,1,4096]{3,0,2,1:T(4,128)S(1)} %multiply_bitcast_fusion.3), channel_id=1, source_target_pairs={{0,8},{8,16},{16,24},{1,9},{9,17},{17,25},{2,10},{10,18},{18,26},{... | collective-permute-start | bytes 147464 | tf_op jit(solution)/shard_map/ppermute | solution.py:19
  132.7 11.8 %collective-permute-start.3 = (f32[3,3,1,4096]{3,2,1,0:T(1,128)S(1)}, f32[3,3,1,4096]{3,2,1,0:T(1,128)S(1)}, u32[]{:S(2)}, u32[]{:S(2)}) collective-permute-start(f32[3,3,1,4096]{3,2,1,0:T(1,128)S(1)} %constant_dynamic-update-slice_fusion), channel_id=1, source_target_pairs={{1,0},{2,1},{3,2},{4,3},{5,4},{6,5},{7,6},{9,8},{10,9},{11,10},{12... | collective-permute-start | bytes 442376 | tf_op jit(solution)/shard_map/ppermute | solution.py:22
  134.0 10.5 %collective-permute-start.2 = (f32[3,3,1,4096]{3,2,1,0:T(1,128)S(1)}, f32[3,3,1,4096]{3,2,1,0:T(1,128)S(1)}, u32[]{:S(2)}, u32[]{:S(2)}) collective-permute-start(f32[3,3,1,4096]{3,2,1,0:T(1,128)S(1)} %constant_dynamic-update-slice_fusion), channel_id=1, source_target_pairs={{0,1},{1,2},{2,3},{3,4},{4,5},{5,6},{6,7},{8,9},{9,10},{10,11},{11... | collective-permute-start | bytes 442376 | tf_op jit(solution)/shard_map/ppermute | solution.py:19
  138.6 9.5 %collective-permute-start.7 = (f32[3,3,1,4096]{3,0,2,1:T(4,128)S(1)}, f32[3,3,1,4096]{3,0,2,1:T(4,128)S(1)}, u32[]{:S(2)}, u32[]{:S(2)}) collective-permute-start(f32[3,3,1,4096]{3,0,2,1:T(4,128)S(1)} %pad_maximum_fusion.5), channel_id=1, source_target_pairs={{1,0},{2,1},{3,2},{4,3},{5,4},{6,5},{7,6},{9,8},{10,9},{11,10},{12... | collective-permute-start | bytes 442376 | tf_op jit(solution)/shard_map/ppermute | solution.py:22
  139.9 11.1 %collective-permute-start.6 = (f32[3,3,1,4096]{3,0,2,1:T(4,128)S(1)}, f32[3,3,1,4096]{3,0,2,1:T(4,128)S(1)}, u32[]{:S(2)}, u32[]{:S(2)}) collective-permute-start(f32[3,3,1,4096]{3,0,2,1:T(4,128)S(1)} %pad_maximum_fusion.5), channel_id=1, source_target_pairs={{0,1},{1,2},{2,3},{3,4},{4,5},{5,6},{6,7},{8,9},{9,10},{10,11},{11... | collective-permute-start | bytes 442376 | tf_op jit(solution)/shard_map/ppermute | solution.py:19
  209.7 4.3 collective-permute-start.9
  211.0 3.9 collective-permute-start.8
  214.9 9.0 %collective-permute-start.11 = (f32[3,3,1,4096]{3,0,2,1:T(4,128)S(1)}, f32[3,3,1,4096]{3,0,2,1:T(4,128)S(1)}, u32[]{:S(2)}, u32[]{:S(2)}) collective-permute-start(f32[3,3,1,4096]{3,0,2,1:T(4,128)S(1)} %pad_maximum_fusion.6), channel_id=1, source_target_pairs={{1,0},{2,1},{3,2},{4,3},{5,4},{6,5},{7,6},{9,8},{10,9},{11,10},{12... | collective-permute-start | bytes 442376 | tf_op jit(solution)/shard_map/ppermute | solution.py:22
  216.2 13.4 %collective-permute-start.10 = (f32[3,3,1,4096]{3,0,2,1:T(4,128)S(1)}, f32[3,3,1,4096]{3,0,2,1:T(4,128)S(1)}, u32[]{:S(2)}, u32[]{:S(2)}) collective-permute-start(f32[3,3,1,4096]{3,0,2,1:T(4,128)S(1)} %pad_maximum_fusion.6), channel_id=1, source_target_pairs={{0,1},{1,2},{2,3},{3,4},{4,5},{5,6},{6,7},{8,9},{9,10},{10,11},{11... | collective-permute-start | bytes 442376 | tf_op jit(solution)/shard_map/ppermute | solution.py:19
  288.3 4.3 collective-permute-start.13
  289.6 3.9 collective-permute-start.12
  293.5 9.0 %collective-permute-start.15 = (f32[3,3,1,4096]{3,0,2,1:T(4,128)S(1)}, f32[3,3,1,4096]{3,0,2,1:T(4,128)S(1)}, u32[]{:S(2)}, u32[]{:S(2)}) collective-permute-start(f32[3,3,1,4096]{3,0,2,1:T(4,128)S(1)} %pad_maximum_fusion.7), channel_id=1, source_target_pairs={{1,0},{2,1},{3,2},{4,3},{5,4},{6,5},{7,6},{9,8},{10,9},{11,10},{12... | collective-permute-start | bytes 442376 | tf_op jit(solution)/shard_map/ppermute | solution.py:22
  294.8 13.4 %collective-permute-start.14 = (f32[3,3,1,4096]{3,0,2,1:T(4,128)S(1)}, f32[3,3,1,4096]{3,0,2,1:T(4,128)S(1)}, u32[]{:S(2)}, u32[]{:S(2)}) collective-permute-start(f32[3,3,1,4096]{3,0,2,1:T(4,128)S(1)} %pad_maximum_fusion.7), channel_id=1, source_target_pairs={{0,1},{1,2},{2,3},{3,4},{4,5},{5,6},{6,7},{8,9},{9,10},{10,11},{11... | collective-permute-start | bytes 442376 | tf_op jit(solution)/shard_map/ppermute | solution.py:19
  366.8 4.3 collective-permute-start.17
  368.1 3.9 collective-permute-start.16
  372.1 9.0 %collective-permute-start.19 = (f32[3,3,1,4096]{3,0,2,1:T(4,128)S(1)}, f32[3,3,1,4096]{3,0,2,1:T(4,128)S(1)}, u32[]{:S(2)}, u32[]{:S(2)}) collective-permute-start(f32[3,3,1,4096]{3,0,2,1:T(4,128)S(1)} %pad_maximum_fusion.8), channel_id=1, source_target_pairs={{1,0},{2,1},{3,2},{4,3},{5,4},{6,5},{7,6},{9,8},{10,9},{11,10},{12... | collective-permute-start | bytes 442376 | tf_op jit(solution)/shard_map/ppermute | solution.py:22
  373.4 13.4 %collective-permute-start.18 = (f32[3,3,1,4096]{3,0,2,1:T(4,128)S(1)}, f32[3,3,1,4096]{3,0,2,1:T(4,128)S(1)}, u32[]{:S(2)}, u32[]{:S(2)}) collective-permute-start(f32[3,3,1,4096]{3,0,2,1:T(4,128)S(1)} %pad_maximum_fusion.8), channel_id=1, source_target_pairs={{0,1},{1,2},{2,3},{3,4},{4,5},{5,6},{6,7},{8,9},{9,10},{10,11},{11... | collective-permute-start | bytes 442376 | tf_op jit(solution)/shard_map/ppermute | solution.py:19
  387.0 58.4 %copy-start.7 = (s32[1,1,16]{2,1,0:T(1,128)S(1)}, s32[1,1,16]{2,1,0:T(1,128)}, u32[]{:S(2)}) copy-start(s32[1,1,16]{2,1,0:T(1,128)} %param.25) | copy-start | bytes 196
  387.0 125.7 %copy-start.1 = (bf16[512,1536]{1,0:T(8,128)(2,1)S(1)}, bf16[512,1536]{1,0:T(8,128)(2,1)}, u32[]{:S(2)}) copy-start(bf16[512,1536]{1,0:T(8,128)(2,1)} %param.19) | copy-start | bytes 4718596
  512.7 2.8 copy-start.4
Sparse Core Ops, SparseCore 0:
  10.2 62.7 all-gather.2
where the time goes:
time: 551 us; the launch traced here: 550 us
  other arithmetic  186 us (34%)
  blocking collectives  107 us (19%)
  waiting for transfers between devices  89.9 us (16%)
  local copies, waits for them, and re-layouts  72.2 us (13%)
  starting transfers between devices  52.1 us (9%)
  matrix products  24.9 us (5%)
  between operations  14.7 us (3%)
    reduce_sum x32, other arithmetic, one_group(): projection = jnp.sum(offsets * near_dipoles[:, :, None, :], axis=0)  87.6 us
    all_gather x1, blocking collectives, on_device(): lax.all_gather(local_targets, ('grp', 'dev'), axis=1, tiled=True)  66.1 us
    reduce_sum x32, other arithmetic, one_group(): jnp.sum(offsets * (projection * inverse_fifth)[None], axis=-1)  64.2 us
    all_gather x1, waiting for transfers between devices, on_device(): gathered = lax.all_gather(left_factor, 'dev', axis=0, tiled=True)  56.4 us
    unnamed x2, blocking collectives  41.1 us
    ppermute x10, starting transfers between devices, padded(): lax.ppermute(lax.slice_in_dim(block, block.shape[dim] - width, None, axis...  39.1 us
    mul x32, other arithmetic, one_group(): projection * inverse_fifth  30.1 us
    unnamed x29, local copies, waits for them, and re-layouts  25.9 us
  transfers between devices with their start and end apart: 21, of which 12 were waited for; matrix products, arithmetic and copies ran while one was open for 4% of the time, Pallas kernels for 0%

commit v1 on v0

v1 whole, which is shorter than its diff:
```python
import functools

import jax
import jax.numpy as jnp
from jax import lax
from jax.experimental import pallas as pl
from jax.experimental.pallas import tpu as pltpu
from jax.sharding import PartitionSpec as P

SWEEPS = 4
COUPLING = 2e-07
SOFTEN = 4e-05
BRICK = 0.1
SLAB = 0.03
REACH = 2
BOTH = ("grp", "dev")
F32 = jnp.float32
BF16 = jnp.bfloat16
FEATS = 32
TERMS = 16
PARTS = 3
VMEM = pl.BlockSpec(memory_space=pltpu.VMEM)
SMEM = pl.BlockSpec(memory_space=pltpu.SMEM)


def shift(block, axis, step):
    count = lax.axis_size(axis)
    pairs = [(i, i + step) for i in range(count) if 0 <= i + step < count]
    return lax.ppermute(block, axis, pairs)


def exchange(block):
    column = jnp.stack([shift(block, "grp", 1), block, shift(block, "grp", -1)])
    return shift(column, "dev", 1), column, shift(column, "dev", -1)


def rounded(value):
    return value.astype(BF16).astype(F32)


def features(coords, own):
    x, y, z = coords
    width = x.shape[1]
    row = lax.broadcasted_iota(jnp.int32, (FEATS, width), 0)
    norm = x * x + y * y + z * z
    if own:
        norm = norm + SOFTEN
    first = 21 if own else 18
    is_norm = (row >= first) & (row < first + 3)
    is_one = (row >= 18) & (row < 24) & ~is_norm
    value = jnp.where(row < 6, x, jnp.where(row < 12, y, jnp.where(row < 18, z, norm)))
    high = rounded(value)
    rest = value - high
    middle = rounded(rest)
    low = rest - middle
    kind = lax.rem(row, 6)
    if own:
        kinds = (0, 0, 1, 0, 2, 1)
    else:
        kinds = (0, 1, 0, 2, 0, 1)
    level = jnp.zeros_like(row)
    for at, which in enumerate(kinds):
        level = jnp.where((row < 18) & (kind == at), which, level)
    level = jnp.where(is_norm, row - first, level)
    part = jnp.where(level == 0, high, jnp.where(level == 1, middle, low))
    if own:
        part = jnp.where(row < 18, -2.0 * part, part)
    part = jnp.where(is_one, 1.0, part)
    part = jnp.where(row < 24, part, 0.0)
    return part.astype(BF16)


def weights_kernel(per_step, blocks, links_ref, coords_ref, out_ref, far_ref, own_ref):
    step = pl.program_id(0)
    region = coords_ref.shape[1]
    width = coords_ref.shape[2]
    listed = out_ref.shape[1] // width
    own_base = region // 9 * 4

    def row_of(at):
        return tuple(coords_ref[k, pl.ds(at, 1), :] for k in range(3))

    @pl.when(step == 0)
    def _():
        def fill(at, carry):
            far_ref[at] = features(row_of(at), False)
            return carry

        lax.fori_loop(0, region, fill, 0, unroll=4)

    diagonal = lax.broadcasted_iota(jnp.int32, (width, width), 0) == lax.broadcasted_iota(
        jnp.int32, (width, width), 1
    )
    for inner in range(per_step):
        block = step * per_step + inner
        x, y, z = row_of(own_base + block)
        for at in range(2 * REACH + 1):
            own_ref[inner, at] = features((x, y, z - (at - REACH) * SLAB), True)
    for inner in range(per_step):
        block = step * per_step + inner
        for n in range(listed):
            link = links_ref[block, n]
            hop = lax.rem(link, blocks) - block + REACH
            square = lax.dot_general(
                far_ref[link],
                own_ref[inner, hop],
                (((0,), (0,)), ((), ())),
                preferred_element_type=F32,
            )
            root = lax.rsqrt(square)
            two = root * root
            value = two * two * root
            if n == 0:
                value = jnp.where(diagonal, 0.0, value)
            out_ref[inner, n * width : (n + 1) * width, :] = value.astype(BF16)


def pair_weights(links, coords, blocks):
    listed = links.shape[1]
    region, width = coords.shape[1:]
    per_step = 2
    return pl.pallas_call(
        functools.partial(weights_kernel, per_step, blocks),
        out_shape=jax.ShapeDtypeStruct((blocks, listed * width, width), BF16),
        grid=(blocks // per_step,),
        in_specs=[SMEM, pl.BlockSpec((3, region, width), lambda i: (0, 0, 0))],
        out_specs=pl.BlockSpec((per_step, listed * width, width), lambda i: (i, 0, 0)),
        scratch_shapes=[
            pltpu.VMEM((region, FEATS, width), BF16),
            pltpu.VMEM((per_step, 2 * REACH + 1, FEATS, width), BF16),
        ],
        name="pair_weights",
    )(links, coords)


def sweep_kernel(
    per_step,
    blocks,
    first,
    last,
    base,
    at_ref,
    links_ref,
    target_ref,
    polar_ref,
    field_ref,
    coords_ref,
    low_ref,
    mid_ref,
    high_ref,
    weights_ref,
    alpha_ref,
    total_ref,
    *rest,
):
    if first:
        out_ref, sum_ref, v_ref, w_ref, p_ref = rest
    elif last:
        out_ref, pick_ref, v_ref, w_ref, p_ref = rest
    else:
        out_ref, v_ref, w_ref, p_ref = rest
    step = pl.program_id(0)
    region, width = coords_ref.shape[1:]
    listed = weights_ref.shape[1] // width
    own_base = 4 * blocks
    lane = lax.broadcasted_iota(jnp.int32, (1, width), 1)

    @pl.when(step == 0)
    def _():
        for a in range(3):
            for b, ref in enumerate((low_ref, mid_ref, high_ref)):
                for k in range(3):
                    v_ref[k, (3 * a + b) * blocks : (3 * a + b + 1) * blocks, :] = ref[
                        a, base + k * blocks : base + (k + 1) * blocks, :
                    ]
        if first:
            per_brick = target_ref.shape[1]
            groups, members = at_ref[2], at_ref[3]
            per_row = field_ref.shape[1] // per_brick
            sum_ref[...] = total_ref[...]

            def brick(p, carry):
                grp = jnp.clip(at_ref[0] + p // 3 - 1, 0, groups - 1)
                dev = jnp.clip(at_ref[1] + p % 3 - 1, 0, members - 1)
                owner = grp * members + dev
                chunk = owner // per_row
                start = owner % per_row * per_brick

                def one(j, inner):
                    site = target_ref[p, j]
                    here = lane == site % width
                    row = p * blocks + site // width
                    for k in range(3):
                        value = field_ref[chunk * 3 + k, start + j]
                        add = jnp.where(here, value * polar_ref[p, j], 0.0)
                        v_ref[k, pl.ds(row, 1), :] += add
                    return inner

                return lax.fori_loop(0, per_brick, one, carry, unroll=4)

            lax.fori_loop(0, 9, brick, 0)
            owner = at_ref[0] * members + at_ref[1]
            chunk = owner // per_row
            start = owner % per_row * per_brick

            def mine(j, carry):
                site = target_ref[4, j]
                here = lane == site % width
                for k in range(3):
                    value = field_ref[chunk * 3 + k, start + j]
                    sum_ref[pl.ds(k * blocks + site // width, 1), :] += jnp.where(here, value, 0.0)
                return carry

            lax.fori_loop(0, per_brick, mine, 0, unroll=4)

    row = lax.broadcasted_iota(jnp.int32, (TERMS, width), 0)
    which = lax.rem(row, 3)
    for inner in range(per_step):
        block = step * per_step + inner
        for n in range(listed):
            link = links_ref[block, n]
            away = (lax.rem(link, blocks) - block).astype(F32) * SLAB
            x = coords_ref[0, pl.ds(link, 1), :]
            y = coords_ref[1, pl.ds(link, 1), :]
            z = coords_ref[2, pl.ds(link, 1), :] + away
            v0, v1, v2 = (v_ref[k, pl.ds(link, 1), :] for k in range(3))
            along = x * v0 + y * v1 + z * v2
            third = (x * x + y * y + z * z) * (1.0 / 3.0)
            dipole = jnp.where(which == 0, v0, jnp.where(which == 1, v1, v2))
            place = jnp.where(
                row < 3,
                1.0,
                jnp.where(
                    (row < 6) | (row == 12), x, jnp.where((row < 9) | (row == 13), y, z)
                ),
            )
            value = jnp.where(row < 12, place * dipole, place * along - third * dipole)
            cols = slice(n * width, (n + 1) * width)
            for part in range(PARTS):
                piece = value.astype(BF16)
                w_ref[inner, part * TERMS : (part + 1) * TERMS, cols] = piece
                if part < PARTS - 1:
                    value = value - piece.astype(F32)
        product = jnp.dot(w_ref[inner], weights_ref[inner], preferred_element_type=F32)
        total = product[:TERMS]
        for part in range(1, PARTS):
            total = total + product[part * TERMS : (part + 1) * TERMS]
        p_ref[block] = total

    @pl.when(step == pl.num_programs(0) - 1)
    def _():
        x = [coords_ref[k, own_base : own_base + blocks, :] for k in range(3)]
        term = [p_ref[:, r, :] for r in range(15)]
        p = term[:3]
        m = [term[3 + 3 * k : 6 + 3 * k] for k in range(3)]
        q = term[12:15]
        inside = x[0] * p[0] + x[1] * p[1] + x[2] * p[2] - (m[0][0] + m[1][1] + m[2][2])
        size = x[0] * x[0] + x[1] * x[1] + x[2] * x[2] + SOFTEN
        alpha = alpha_ref[...]
        for k in range(3):
            one = x[0] * m[k][0] + x[1] * m[k][1] + x[2] * m[k][2]
            other = x[0] * m[0][k] + x[1] * m[1][k] + x[2] * m[2][k]
            force = x[k] * inside - one + q[k] - (size * p[k] - 2.0 * other) * (1.0 / 3.0)
            rows = slice(k * blocks, (k + 1) * blocks)
            given = sum_ref[rows, :] if first else total_ref[rows, :]
            out_ref[rows, :] = alpha * (given + (3.0 * COUPLING) * force)
        if last:
            per_brick = target_ref.shape[1]
            pick_ref[...] = jnp.zeros_like(pick_ref)

            def pick(j, carry):
                site = target_ref[4, j]
                here = lane == site % width
                line = jnp.zeros((1, width), F32)
                for k in range(3):
                    values = out_ref[pl.ds(k * blocks + site // width, 1), :]
                    found = jnp.sum(jnp.where(here, values, 0.0), axis=1, keepdims=True)
                    line = jnp.where(lane == k, found, line)
                pick_ref[pl.ds(j, 1), :] = line
                return carry

            lax.fori_loop(0, per_brick, pick, 0, unroll=True)


def sweep(at, links, targets, polar, field, coords, around, weights, alpha, total, first, last, base):
    blocks, depth, width = weights.shape
    region = coords.shape[1]
    per_step = 4
    outs = [jax.ShapeDtypeStruct((3 * blocks, width), F32)]
    if first:
        outs.append(jax.ShapeDtypeStruct((3 * blocks, width), F32))
    if last:
        outs.append(jax.ShapeDtypeStruct((targets.shape[1], width), F32))

    def whole(array):
        return pl.BlockSpec(array.shape, lambda i: (0,) * len(array.shape))

    return pl.pallas_call(
        functools.partial(sweep_kernel, per_step, blocks, first, last, base),
        out_shape=outs,
        grid=(blocks // per_step,),
        in_specs=[
            SMEM,
            SMEM,
            SMEM,
            SMEM,
            SMEM,
            whole(coords),
            whole(around[0]),
            whole(around[1]),
            whole(around[2]),
            pl.BlockSpec((per_step, depth, width), lambda i: (i, 0, 0)),
            whole(alpha),
            whole(total),
        ],
        out_specs=[whole(o) for o in outs],
        scratch_shapes=[
            pltpu.VMEM((3, region, width), F32),
            pltpu.VMEM((per_step, PARTS * TERMS, depth), BF16),
            pltpu.VMEM((blocks, TERMS, width), F32),
        ],
        name="sweep",
    )(at, links, targets, polar, field, coords, *around, weights, alpha, total)


def context_kernel(count, source_ref, *refs):
    lefts = refs[:count]
    density_ref = refs[count]
    rights = refs[count + 1 : 2 * count + 1]
    directions_ref, out_ref, left_ref, sums_ref = refs[2 * count + 1 :]
    step = pl.program_id(0)
    rows = lefts[0].shape[0]

    @pl.when(step == 0)
    def _():
        for i, ref in enumerate(lefts):
            left_ref[i * rows : (i + 1) * rows, :] = ref[...]
        sums_ref[...] = jnp.zeros_like(sums_ref)

    context = jnp.dot(left_ref[...], density_ref[...], preferred_element_type=F32)
    lanes = context.shape[1]
    for i, ref in enumerate(rights):
        weighted = context[i * rows : (i + 1) * rows] * ref[...].astype(F32)
        for k in range(3):
            term = weighted * directions_ref[k : k + 1, :]
            folded = term[:, :128]
            for at in range(128, lanes, 128):
                folded = folded + term[:, at : at + 128]
            sums_ref[k, i * rows : (i + 1) * rows, :] += folded

    @pl.when(step == pl.num_programs(0) - 1)
    def _():
        for k in range(3):
            for at in range(0, sums_ref.shape[1], 128):
                flipped = jnp.transpose(sums_ref[k, at : at + 128, :])
                out_ref[k : k + 1, at : at + 128] = jnp.sum(flipped, axis=0, keepdims=True)


def context_field(sources, chunks, density, right, directions):
    count = len(chunks)
    rows, depth = chunks[0].shape
    columns = density.shape[1]
    tile = 256
    padded = -(-count * rows // 128) * 128

    def right_block(i):
        return pl.BlockSpec((rows, tile), lambda j, source: (source[i], j))

    return pl.pallas_call(
        functools.partial(context_kernel, count),
        out_shape=jax.ShapeDtypeStruct((3, padded), F32),
        grid_spec=pltpu.PrefetchScalarGridSpec(
            num_scalar_prefetch=1,
            grid=(columns // tile,),
            in_specs=[pl.BlockSpec((rows, depth), lambda j, source: (0, 0)) for _ in chunks]
            + [pl.BlockSpec((depth, tile), lambda j, source: (0, j))]
            + [right_block(i) for i in range(count)]
            + [pl.BlockSpec((3, tile), lambda j, source: (0, j))],
            out_specs=pl.BlockSpec((3, padded), lambda j, source: (0, 0)),
            scratch_shapes=[
                pltpu.VMEM((count * rows, depth), BF16),
                pltpu.VMEM((3, padded, 128), F32),
            ],
        ),
        name="context_field",
    )(sources, *chunks, density, *([right] * count), directions)


def fock_kernel(count, source_ref, *refs):
    lefts = refs[:count]
    right_ref, directions_ref, dipoles_ref, out_ref, scaled_ref = refs[count:]
    rows = lefts[0].shape[0]

    @pl.when(pl.program_id(0) == 0)
    def _():
        lines = [directions_ref[k : k + 1, :] for k in range(3)]
        for i in range(count):
            start = pl.multiple_of(source_ref[i] * rows, rows)
            dipoles = dipoles_ref[pl.ds(start, rows), :]
            along = dipoles[:, 0:1] * lines[0]
            for k in (1, 2):
                along = along + dipoles[:, k : k + 1] * lines[k]
            value = right_ref[pl.ds(start, rows), :].astype(F32) * along
            scaled_ref[i * rows : (i + 1) * rows, :] = (-value).astype(BF16)

    left = jnp.concatenate([ref[...] for ref in lefts], axis=0)
    out_ref[...] = lax.dot_general(
        left, scaled_ref[...], (((0,), (0,)), ((), ())), preferred_element_type=F32
    )


def fock_term(sources, chunks, right, directions, dipoles):
    count = len(chunks)
    rows, depth = chunks[0].shape
    targets, columns = right.shape
    tile = 512

    def whole(array):
        return pl.BlockSpec(array.shape, lambda i, source: (0,) * len(array.shape))

    return pl.pallas_call(
        functools.partial(fock_kernel, count),
        out_shape=jax.ShapeDtypeStruct((depth, columns), F32),
        grid_spec=pltpu.PrefetchScalarGridSpec(
            num_scalar_prefetch=1,
            grid=(depth // tile,),
            in_specs=[pl.BlockSpec((rows, tile), lambda i, source: (0, i)) for _ in chunks]
            + [whole(right), whole(directions), whole(dipoles)],
            out_specs=pl.BlockSpec((tile, columns), lambda i, source: (i, 0)),
            scratch_shapes=[pltpu.VMEM((targets, columns), BF16)],
        ),
        name="fock_term",
    )(sources, *chunks, right, directions, dipoles)


def ring_order(count):
    return list(range(0, count, 2)) + [i for i in range(count - 1, 0, -1) if i % 2]


def on_device(
    density, left_factor, right_factor, directions, places, alpha, static_field, neighbours, targets
):
    groups = lax.axis_size("grp")
    members = lax.axis_size("dev")
    grp = lax.axis_index("grp")
    dev = lax.axis_index("dev")
    rows = left_factor.shape[0]
    per_brick = targets.shape[2]
    sites = places.shape[3]
    blocks = neighbours.shape[2]
    width = sites // blocks
    devices = groups * members

    links = neighbours[0, 0]
    polar = alpha[0, 0]
    own_targets = targets[0, 0]
    fixed = static_field[:, 0, 0]
    picked = jnp.sum(
        jnp.where(own_targets[:, None] == jnp.arange(sites, dtype=jnp.int32)[None, :], polar[None, :], 0.0),
        axis=1,
    )
    tail = jnp.zeros((8, width), F32)
    tail = tail.at[0, :per_brick].set(own_targets.astype(F32)).at[1, :per_brick].set(picked)
    packed = jnp.concatenate(
        [
            places[:, 0, 0].reshape(3 * blocks, width),
            (polar[None] * fixed).reshape(3 * blocks, width),
            tail,
        ]
    )
    around = exchange(packed)
    everything = jnp.stack(around, axis=1).reshape(9, packed.shape[0], width)
    region = everything[:, : 3 * blocks].reshape(9, 3, blocks, width).transpose(1, 0, 2, 3)
    region = region.reshape(3, 9 * blocks, width)
    level = (jnp.arange(9 * blocks, dtype=jnp.int32) % blocks).astype(F32)
    middle_x = (grp.astype(F32) + 0.5) * BRICK
    middle_y = (dev.astype(F32) + 0.5) * BRICK
    middle_z = (level + 0.5) * SLAB
    coords = jnp.stack([region[0] - middle_x, region[1] - middle_y, region[2] - middle_z[:, None]])
    nearby_targets = everything[:, 6 * blocks, :per_brick].astype(jnp.int32)
    nearby_polar = everything[:, 6 * blocks + 1, :per_brick]
    weights = pair_weights(links, coords, blocks)

    order = ring_order(members)
    place_of = [order.index(i) for i in range(members)]
    order_table = jnp.array(order, jnp.int32)
    position = jnp.array(place_of, jnp.int32)[dev]
    forward = [(order[i], order[(i + 1) % members]) for i in range(members)]
    backward = [(b, a) for a, b in forward]
    chunks = {0: left_factor}
    onward = back = left_factor
    groups_of = [[0]]
    for step in range(1, members // 2 + 1):
        onward = lax.ppermute(onward, "dev", forward)
        chunks[-step] = onward
        fresh = [-step]
        if step <= (members - 1) // 2:
            back = lax.ppermute(back, "dev", backward)
            chunks[step] = back
            fresh.append(step)
        groups_of.append(fresh)
    if len(groups_of) > 1:
        groups_of = [groups_of[0] + groups_of[1]] + groups_of[2:]
    if len(groups_of) > 2 and len(groups_of[-1]) == 1:
        groups_of = groups_of[:-2] + [groups_of[-2] + groups_of[-1]]

    def source_of(offset):
        return order_table[lax.rem(position + offset + members, members)]

    fields = {}
    for offsets in groups_of:
        sources = jnp.stack([source_of(o) for o in offsets])
        part = context_field(sources, [chunks[o] for o in offsets], density, right_factor, directions)
        for i, offset in enumerate(offsets):
            fields[offset % members] = part[:, i * rows : (i + 1) * rows]
    by_offset = jnp.stack([fields[o] for o in range(members)])
    back_offset = lax.rem(jnp.array(place_of, jnp.int32) - position + members, members)
    partial = jnp.take(by_offset, back_offset, axis=0).reshape(members * 3, rows)
    spread = jnp.broadcast_to(partial[None], (devices,) + partial.shape)
    field = jnp.sum(lax.all_to_all(spread, BOTH, 0, 0), axis=0)
    owner = grp * members + dev
    local = lax.dynamic_slice_in_dim(field.reshape(members, 3, rows), owner * per_brick // rows, 1, 0)
    qm_local = lax.dynamic_slice_in_dim(local[0], owner * per_brick % rows, per_brick, 1)

    at = jnp.stack([grp, dev, jnp.int32(groups), jnp.int32(members)]).astype(jnp.int32)
    alpha_rows = polar.reshape(blocks, width)
    total = fixed.reshape(3 * blocks, width)
    picks = None
    for repeat in range(SWEEPS):
        first, last = repeat == 0, repeat == SWEEPS - 1
        result = sweep(
            at,
            links,
            nearby_targets,
            nearby_polar,
            field,
            coords,
            around,
            weights,
            alpha_rows,
            total,
            first,
            last,
            3 * blocks if first else 0,
        )
        current = result[0]
        if first:
            total = result[1]
        if last:
            picks = result[1]
        else:
            around = exchange(current)
    spread = jnp.broadcast_to(picks[None], (devices,) + picks.shape)
    dipoles = lax.all_to_all(spread, BOTH, 0, 0).reshape(devices * per_brick, width)
    offsets = sorted(chunks)
    sources = jnp.stack([source_of(o) for o in offsets])
    fock_polar = fock_term(sources, [chunks[o] for o in offsets], right_factor, directions, dipoles)
    return (current.reshape(3, 1, 1, sites), qm_local, fock_polar)


def solution(mesh):
    placed = (
        P("grp", "dev"),
        P("dev", "grp"),
        P(None, "dev"),
        P(None, "dev"),
        P(None, "grp", "dev", None),
        P("grp", "dev", None),
        P(None, "grp", "dev", None),
        P("grp", "dev", None, None),
        P("grp", "dev", None),
    )
    return jax.shard_map(
        on_device,
        mesh=mesh,
        in_specs=placed,
        out_specs=(P(None, "grp", "dev", None), P(None, ("grp", "dev")), P("grp", "dev")),
        check_vma=False,
    )
```

time: 551 us -> 250 us (0.45)
  other arithmetic: 186 us -> 17.4 us
  blocking collectives: 107 us -> 0 us
  Pallas kernels: 0 us -> 98.5 us
  local copies, waits for them, and re-layouts: 72.2 us -> 23.2 us
  waiting for transfers between devices: 89.9 us -> 41.8 us
  matrix products: 24.9 us -> 0 us
  starting transfers between devices: 52.1 us -> 60.7 us
  between operations: 14.7 us -> 6.39 us
    reduce_sum x64 -> x2, other arithmetic: 152 us -> 1.57 us  [the longest x1 0.93 us: on_device(): jnp.sum(jnp.where(own_targets[:, None] == jnp.arange(sites, dtype=jnp.int...]
    pallas_call x0 -> x9, Pallas kernels: none -> 98.5 us  [the longest x4 44.5 us: sweep(): pl.pallas_call(functools.partial(sweep_kernel, per_step, blocks, first, l...]
    all_gather x1 -> x0, blocking collectives: 66.1 us -> none  [on_device(): lax.all_gather(local_targets, ('grp', 'dev'), axis=1, tiled=True)]
    all_gather x1 -> x0, waiting for transfers between devices: 56.4 us -> none  [on_device(): gathered = lax.all_gather(left_factor, 'dev', axis=0, tiled=True)]
    unnamed x2 -> x0, blocking collectives: 41.1 us -> none
    gather x128 -> x2, local copies, waits for them, and re-layouts: 41.1 us -> 0.59 us  [on_device(): jnp.take(by_offset, back_offset, axis=0).reshape(members * 3, rows)]
    mul x32 -> x2, other arithmetic: 30.1 us -> 0.82 us  [the longest x1 0.81 us: on_device(): polar[None] * fixed]
    dot_general x6 -> x0, matrix products: 24.9 us -> none  [the longest x1 9.63 us: on_device(): context = jnp.dot(gathered, density, preferred_element_type=jnp.float32)]
  transfers between devices with their start and end apart: 21 -> 25, of which waited for: 12 -> 12; matrix products, arithmetic and copies ran while one was open for 4% -> 9% of each run, Pallas kernels for 0% -> 13%
where the time goes in v1:
time: 250 us; the launch traced here: 248 us
  Pallas kernels  98.5 us (39%)
  starting transfers between devices  60.7 us (24%)
  waiting for transfers between devices  41.8 us (17%)
  local copies, waits for them, and re-layouts  23.2 us (9%)
  other arithmetic  17.4 us (7%)
  between operations  6.39 us (3%)
    pallas_call x4, Pallas kernels, sweep(): pl.pallas_call(functools.partial(sweep_kernel, per_step, blocks, first, l...  44.5 us
    ppermute x16, starting transfers between devices, shift(): return lax.ppermute(block, axis, pairs)  41.7 us
    pallas_call x3, Pallas kernels, context_field(): pl.pallas_call(functools.partial(context_kernel, count), out_shape=jax.Sh...  25.3 us
    ppermute x16, waiting for transfers between devices, shift(): return lax.ppermute(block, axis, pairs)  22 us
    pallas_call x1, Pallas kernels, pair_weights(): pl.pallas_call(functools.partial(weights_kernel, per_step, blocks), out_s...  15.4 us
    pallas_call x1, Pallas kernels, fock_term(): pl.pallas_call(functools.partial(fock_kernel, count), out_shape=jax.Shape...  13.3 us
    unnamed x56, local copies, waits for them, and re-layouts  11.1 us
    ppermute x3, waiting for transfers between devices, on_device(): back = lax.ppermute(back, 'dev', backward)  7.92 us
  transfers between devices with their start and end apart: 25, of which 12 were waited for; matrix products, arithmetic and copies ran while one was open for 9% of the time, Pallas kernels for 13%

profile of v1, /device:TPU:0, one launch (start us, length us, event | category | flops | bytes accessed | tf_op | source)
XLA Modules:
  0.0 247.9 jit_solution(13181171265804229511)
XLA Ops:
  4.0 1.3 collective-permute-start.1
  5.3 3.0 %collective-permute-start = (f32[200,128]{1,0:T(8,128)S(1)}, f32[200,128]{1,0:T(8,128)S(1)}, u32[]{:S(2)}, u32[]{:S(2)}) collective-permute-start(f32[200,128]{1,0:T(8,128)S(1)} %get-tuple-element.54), channel_id=1, source_target_pairs={{0,8},{8,16},{16,24},{1,9},{9,17},{17,25},{2,10},{10,18},{18,26},{... | collective-permute-start | bytes 307208 | tf_op jit(solution)/shard_map/ppermute | solution.py:29
  8.3 3.0 %collective-permute-start.5 = (bf16[64,3072]{1,0:T(8,128)(2,1)}, bf16[64,3072]{1,0:T(8,128)(2,1)S(1)}, u32[]{:S(2)}, u32[]{:S(2)}) collective-permute-start(bf16[64,3072]{1,0:T(8,128)(2,1)} %refs_4_.7), channel_id=1, source_target_pairs={{2,0},{4,2},{6,4},{7,6},{5,7},{3,5},{1,3},{0,1},{10,8},{12,10},{14... | collective-permute-start | bytes 1179656 | tf_op jit(solution)/shard_map/ppermute | solution.py:498
  11.5 1.2 dynamic_slice.41
  18.1 1.6 fusion.11
  19.7 4.3 %pad_add_fusion.1 = (s32[3]{0:T(128)}, s32[3]{0:T(128)}) fusion(s32[1]{0:T(128)} %get-tuple-element.58, s32[1]{0:T(128)} %get-tuple-element.59, s32[1]{0:T(128)} %get-tuple-element.60, s32[1]{0:T(128)} %get-tuple-element.61, s32[1]{0:T(128)} %get-tuple-element.62, s32[1]{0:T(128)} %get-tuple-element.55), kind=kLoop, calls=%fused_computation.49 | loop fusion | flops 12 | bytes 48 | tf_op jit(solution)/shard_map/stack | solution.py:512
  24.0 1.3 compare_and_fusion
  25.4 1.9 pad_add_fusion.2.source_ref
  27.3 2.0 collective-permute-start.6
  30.1 1.4 copy.25
  31.6 1.3 collective-permute-start.3
  32.9 4.6 %collective-permute-start.2 = (f32[3,200,128]{2,1,0:T(8,128)S(1)}, f32[3,200,128]{2,1,0:T(8,128)S(1)}, u32[]{:S(2)}, u32[]{:S(2)}) collective-permute-start(f32[3,200,128]{2,1,0:T(8,128)S(1)} %get-tuple-element.52.mid_ref), channel_id=1, source_target_pairs={{0,1},{1,2},{2,3},{3,4},{4,5},{5,6},{6,7},{8,9},{9,10},{10,11},{11... | collective-permute-start | bytes 921608 | tf_op jit(solution)/shard_map/ppermute | solution.py:29
  38.2 8.6 %context_field.3 = f32[3,256]{1,0:T(4,128)} custom-call(s32[3]{0:T(128)} %get-tuple-element.65.source_ref, bf16[64,3072]{1,0:T(8,128)(2,1)} %refs_4_.7, bf16[64,3072]{1,0:T(8,128)(2,1)} %copy-done.3, bf16[64,3072]{1,0:T(8,128)(2,1)} %copy-done.2, bf16[3072,1536]{1,0:T(8,128)(2,1)} %refs_3_.5, bf16[512,1536]{1,0:T(8,128)(2,1)} %refs_8_.1, ...), custom_call_target="tpu_custom_call" | custom-call | tf_op jit(solution)/shard_map/context_field/pallas_call | solution.py:369
  50.5 7.9 %collective-permute-done.7.refs_1_.refs_6_ = bf16[64,3072]{1,0:T(8,128)(2,1)S(1)} collective-permute-done((bf16[64,3072]{1,0:T(8,128)(2,1)}, bf16[64,3072]{1,0:T(8,128)(2,1)S(1)}, u32[]{:S(2)}, u32[]{:S(2)}) %collective-permute-start.7) | collective-permute-done | bytes 393248 | tf_op jit(solution)/shard_map/ppermute | solution.py:498
  58.4 1.3 collective-permute-start.9
  61.4 15.4 %pair_weights.1.weights_ref = bf16[32,1536,128]{2,1,0:T(8,128)(2,1)} custom-call(s32[32,12]{1,0:T(8,128)} %bitcast.83, f32[3,288,128]{2,1,0:T(8,128)} %pad_maximum_fusion.1.coords_ref), custom_call_target="tpu_custom_call" | custom-call | tf_op jit(solution)/shard_map/pair_weights/pallas_call | solution.py:122
  76.8 8.1 %context_field.4 = f32[3,128]{1,0:T(4,128)} custom-call(s32[2]{0:T(128)} %pad_add_fusion.2.source_ref, bf16[64,3072]{1,0:T(8,128)(2,1)} %copy-done, bf16[64,3072]{1,0:T(8,128)(2,1)} %copy-done.1, bf16[3072,1536]{1,0:T(8,128)(2,1)} %refs_3_.5, bf16[512,1536]{1,0:T(8,128)(2,1)} %refs_8_.1, bf16[512,1536]{1,0:T(8,128)(2,1)} %refs_8_.1, f32[3,1536]{1,0:T(4,128)} %refs_9_.1), custom_call_target="tpu_custom_call" | custom-call | tf_op jit(solution)/shard_map/context_field/pallas_call | solution.py:369
  86.7 8.6 %context_field.5 = f32[3,256]{1,0:T(4,128)} custom-call(s32[3]{0:T(128)} %get-tuple-element.66.source_ref, bf16[64,3072]{1,0:T(8,128)(2,1)} %copy-done.4, bf16[64,3072]{1,0:T(8,128)(2,1)} %copy-done.5, bf16[64,3072]{1,0:T(8,128)(2,1)} %copy-done.6, bf16[3072,1536]{1,0:T(8,128)(2,1)} %refs_3_.5, bf16[512,1536]{1,0:T(8,128)(2,1)} %refs_8_.1, ...), custom_call_target="tpu_custom_call" | custom-call | tf_op jit(solution)/shard_map/context_field/pallas_call | solution.py:369
  99.1 4.0 %all-to-all-start = ((f32[32,1,1536]{2,1,0:T(1,128)}), f32[32,1,1536]{2,1,0:T(1,128)S(1)}, u32[]{:S(2)}, u32[]{:S(2)}) async-start(f32[32,1,1536]{2,1,0:T(1,128)} %reshape.200), calls=%async_computation | async-start | bytes 393216 | tf_op jit(solution)/shard_map/all_to_all | solution.py:520
  103.7 7.6 %all-to-all-done = f32[32,1,1536]{2,1,0:T(1,128)S(1)} async-done(((f32[32,1,1536]{2,1,0:T(1,128)}), f32[32,1,1536]{2,1,0:T(1,128)S(1)}, u32[]{:S(2)}, u32[]{:S(2)}) %all-to-all-start) | async-done | bytes 196640 | tf_op jit(solution)/shard_map/all_to_all | solution.py:520
  111.8 1.1 reduce.4
  113.7 13.2 %sweep.4 = (f32[96,128]{1,0:T(8,128)}, f32[96,128]{1,0:T(8,128)}) custom-call(s32[4]{0:T(128)} %pad_add_fusion.at_ref, s32[32,12]{1,0:T(8,128)} %bitcast.84, s32[9,16]{1,0:T(8,128)} %get-tuple-element.64.target_ref, f32[9,16]{1,0:T(8,128)} %get-tuple-element.63.polar_ref, f32[24,64]{1,0:T(8,128)} %reduce_sum.19.field_ref, ...), custom_call_target="tpu_custom_call" | custom-call | tf_op jit(solution)/shard_map/sweep/pallas_call | solution.py:298
  126.8 1.3 collective-permute-start.12
  128.1 3.0 %collective-permute-start.11 = (f32[96,128]{1,0:T(8,128)}, f32[96,128]{1,0:T(8,128)S(1)}, u32[]{:S(2)}, u32[]{:S(2)}) collective-permute-start(f32[96,128]{1,0:T(8,128)} %get-tuple-element.31), channel_id=1, source_target_pairs={{0,8},{8,16},{16,24},{1,9},{9,17},{17,25},{2,10},{10,18},{18,26},{... | collective-permute-start | bytes 147464 | tf_op jit(solution)/shard_map/ppermute | solution.py:29
  133.1 1.3 collective-permute-start.14
  134.4 4.6 %collective-permute-start.13 = (f32[3,96,128]{2,1,0:T(8,128)S(1)}, f32[3,96,128]{2,1,0:T(8,128)S(1)}, u32[]{:S(2)}, u32[]{:S(2)}) collective-permute-start(f32[3,96,128]{2,1,0:T(8,128)S(1)} %pad_maximum_fusion.3.mid_ref), channel_id=1, source_target_pairs={{0,1},{1,2},{2,3},{3,4},{4,5},{5,6},{6,7},{8,9},{9,10},{10,11},{11... | collective-permute-start | bytes 442376 | tf_op jit(solution)/shard_map/ppermute | solution.py:29
  138.9 1.6 collective-permute-done.14.high_ref
  140.6 4.6 %collective-permute-done.13.low_ref = f32[3,96,128]{2,1,0:T(8,128)S(1)} collective-permute-done((f32[3,96,128]{2,1,0:T(8,128)S(1)}, f32[3,96,128]{2,1,0:T(8,128)S(1)}, u32[]{:S(2)}, u32[]{:S(2)}) %collective-permute-start.13) | collective-permute-done | bytes 147488 | tf_op jit(solution)/shard_map/ppermute | solution.py:29
  145.8 10.4 %sweep.5 = f32[96,128]{1,0:T(8,128)} custom-call(s32[4]{0:T(128)} %pad_add_fusion.at_ref, s32[32,12]{1,0:T(8,128)} %bitcast.85, s32[9,16]{1,0:T(8,128)} %get-tuple-element.64.target_ref, f32[9,16]{1,0:T(8,128)} %get-tuple-element.63.polar_ref, f32[24,64]{1,0:T(8,128)} %reduce_sum.19.field_ref, f32[3,288,128]{2,1,0:T(8,128)} %pad_maximum_fusion.1.coords_ref, ...), custom_call_target="tpu_custom_call" | custom-call | tf_op jit(solution)/shard_map/sweep/pallas_call | solution.py:298
  156.2 1.3 collective-permute-start.16
  157.5 3.0 %collective-permute-start.15 = (f32[96,128]{1,0:T(8,128)}, f32[96,128]{1,0:T(8,128)S(1)}, u32[]{:S(2)}, u32[]{:S(2)}) collective-permute-start(f32[96,128]{1,0:T(8,128)} %sweep.5), channel_id=1, source_target_pairs={{0,8},{8,16},{16,24},{1,9},{9,17},{17,25},{2,10},{10,18},{18,26},{... | collective-permute-start | bytes 147464 | tf_op jit(solution)/shard_map/ppermute | solution.py:29
  162.4 1.4 collective-permute-start.18
  163.9 5.0 %collective-permute-start.17 = (f32[3,96,128]{2,1,0:T(8,128)S(1)}, f32[3,96,128]{2,1,0:T(8,128)S(1)}, u32[]{:S(2)}, u32[]{:S(2)}) collective-permute-start(f32[3,96,128]{2,1,0:T(8,128)S(1)} %pad_maximum_fusion.4.mid_ref), channel_id=1, source_target_pairs={{0,1},{1,2},{2,3},{3,4},{4,5},{5,6},{6,7},{8,9},{9,10},{10,11},{11... | collective-permute-start | bytes 442376 | tf_op jit(solution)/shard_map/ppermute | solution.py:29
  168.9 1.7 collective-permute-done.18.high_ref
  170.6 4.6 %collective-permute-done.17.low_ref = f32[3,96,128]{2,1,0:T(8,128)S(1)} collective-permute-done((f32[3,96,128]{2,1,0:T(8,128)S(1)}, f32[3,96,128]{2,1,0:T(8,128)S(1)}, u32[]{:S(2)}, u32[]{:S(2)}) %collective-permute-start.17) | collective-permute-done | bytes 147488 | tf_op jit(solution)/shard_map/ppermute | solution.py:29
  175.9 10.4 %sweep.6 = f32[96,128]{1,0:T(8,128)} custom-call(s32[4]{0:T(128)} %pad_add_fusion.at_ref, s32[32,12]{1,0:T(8,128)} %bitcast.86, s32[9,16]{1,0:T(8,128)} %get-tuple-element.64.target_ref, f32[9,16]{1,0:T(8,128)} %get-tuple-element.63.polar_ref, f32[24,64]{1,0:T(8,128)} %reduce_sum.19.field_ref, f32[3,288,128]{2,1,0:T(8,128)} %pad_maximum_fusion.1.coords_ref, ...), custom_call_target="tpu_custom_call" | custom-call | tf_op jit(solution)/shard_map/sweep/pallas_call | solution.py:298
  186.2 1.3 collective-permute-start.20
  187.5 3.0 %collective-permute-start.19 = (f32[96,128]{1,0:T(8,128)}, f32[96,128]{1,0:T(8,128)S(1)}, u32[]{:S(2)}, u32[]{:S(2)}) collective-permute-start(f32[96,128]{1,0:T(8,128)} %sweep.6), channel_id=1, source_target_pairs={{0,8},{8,16},{16,24},{1,9},{9,17},{17,25},{2,10},{10,18},{18,26},{... | collective-permute-start | bytes 147464 | tf_op jit(solution)/shard_map/ppermute | solution.py:29
  192.5 1.3 collective-permute-start.22
  193.8 5.0 %collective-permute-start.21 = (f32[3,96,128]{2,1,0:T(8,128)S(1)}, f32[3,96,128]{2,1,0:T(8,128)S(1)}, u32[]{:S(2)}, u32[]{:S(2)}) collective-permute-start(f32[3,96,128]{2,1,0:T(8,128)S(1)} %pad_maximum_fusion.5.mid_ref), channel_id=1, source_target_pairs={{0,1},{1,2},{2,3},{3,4},{4,5},{5,6},{6,7},{8,9},{9,10},{10,11},{11... | collective-permute-start | bytes 442376 | tf_op jit(solution)/shard_map/ppermute | solution.py:29
  198.8 1.7 collective-permute-done.22.high_ref
  200.5 4.6 %collective-permute-done.21.low_ref = f32[3,96,128]{2,1,0:T(8,128)S(1)} collective-permute-done((f32[3,96,128]{2,1,0:T(8,128)S(1)}, f32[3,96,128]{2,1,0:T(8,128)S(1)}, u32[]{:S(2)}, u32[]{:S(2)}) %collective-permute-start.21) | collective-permute-done | bytes 147488 | tf_op jit(solution)/shard_map/ppermute | solution.py:29
  205.7 10.6 %sweep.7 = (f32[96,128]{1,0:T(8,128)}, f32[16,128]{1,0:T(8,128)}) custom-call(s32[4]{0:T(128)} %pad_add_fusion.at_ref, s32[32,12]{1,0:T(8,128)} %bitcast.87, s32[9,16]{1,0:T(8,128)} %get-tuple-element.64.target_ref, f32[9,16]{1,0:T(8,128)} %get-tuple-element.63.polar_ref, f32[24,64]{1,0:T(8,128)} %reduce_sum.19.field_ref, ...), custom_call_target="tpu_custom_call" | custom-call | tf_op jit(solution)/shard_map/sweep/pallas_call | solution.py:298
  216.3 1.4 broadcast_in_dim.50
  217.7 5.7 %all-to-all-start.1 = ((f32[32,16,128]{2,1,0:T(8,128)}), f32[32,16,128]{2,1,0:T(8,128)S(1)}, u32[]{:S(2)}, u32[]{:S(2)}) async-start(f32[32,16,128]{2,1,0:T(8,128)} %broadcast_in_dim.50), calls=%async_computation.1 | async-start | bytes 524288 | tf_op jit(solution)/shard_map/all_to_all | solution.py:554
  223.4 5.5 %stack.150.source_ref = s32[8]{0:T(128)} concatenate(s32[1]{0:T(128)} %get-tuple-element.61, s32[1]{0:T(128)} %get-tuple-element.55, s32[1]{0:T(128)} %get-tuple-element.57, s32[1]{0:T(128)} %get-tuple-element.59, s32[1]{0:T(128)} %get-tuple-element.60, s32[1]{0:T(128)} %get-tuple-element.58, s32[1]{0:T(128)} %get-tuple-element.56, s32[1]{0:T(128)} %get-tuple-element.62), dimensions={0} | concatenate | bytes 64 | tf_op jit(solution)/shard_map/stack | solution.py:556
  229.6 4.2 %all-to-all-done.1 = f32[32,16,128]{2,1,0:T(8,128)S(1)} async-done(((f32[32,16,128]{2,1,0:T(8,128)}), f32[32,16,128]{2,1,0:T(8,128)S(1)}, u32[]{:S(2)}, u32[]{:S(2)}) %all-to-all-start.1) | async-done | bytes 262176 | tf_op jit(solution)/shard_map/all_to_all | solution.py:554
  234.6 13.3 %fock_term.1 = f32[3072,1536]{1,0:T(8,128)} custom-call(s32[8]{0:T(128)} %stack.150.source_ref, bf16[64,3072]{1,0:T(8,128)(2,1)} %copy-done.6, bf16[64,3072]{1,0:T(8,128)(2,1)} %copy-done.4, bf16[64,3072]{1,0:T(8,128)(2,1)} %copy-done, bf16[64,3072]{1,0:T(8,128)(2,1)} %copy-done.3, bf16[64,3072]{1,0:T(8,128)(2,1)} %refs_4_.7, bf16[64,3072]{1,0:T(8,128)(2,1)} %copy-done.2, ...), custom_call_target="tpu_custom_call" | custom-call | tf_op jit(solution)/shard_map/fock_term/pallas_call | solution.py:421
  (108 shorter events, 26.8 us)
Async XLA Ops:
  4.0 27.5 %collective-permute-start.1 = (f32[200,128]{1,0:T(8,128)S(1)}, f32[200,128]{1,0:T(8,128)S(1)}, u32[]{:S(2)}, u32[]{:S(2)}) collective-permute-start(f32[200,128]{1,0:T(8,128)S(1)} %get-tuple-element.54), channel_id=1, source_target_pairs={{8,0},{16,8},{24,16},{9,1},{17,9},{25,17},{10,2},{18,10},{26,18},{... | collective-permute-start | bytes 307208 | tf_op jit(solution)/shard_map/ppermute | solution.py:29
  5.3 26.2 %collective-permute-start = (f32[200,128]{1,0:T(8,128)S(1)}, f32[200,128]{1,0:T(8,128)S(1)}, u32[]{:S(2)}, u32[]{:S(2)}) collective-permute-start(f32[200,128]{1,0:T(8,128)S(1)} %get-tuple-element.54), channel_id=1, source_target_pairs={{0,8},{8,16},{16,24},{1,9},{9,17},{17,25},{2,10},{10,18},{18,26},{... | collective-permute-start | bytes 307208 | tf_op jit(solution)/shard_map/ppermute | solution.py:29
  8.3 29.1 %collective-permute-start.5 = (bf16[64,3072]{1,0:T(8,128)(2,1)}, bf16[64,3072]{1,0:T(8,128)(2,1)S(1)}, u32[]{:S(2)}, u32[]{:S(2)}) collective-permute-start(bf16[64,3072]{1,0:T(8,128)(2,1)} %refs_4_.7), channel_id=1, source_target_pairs={{2,0},{4,2},{6,4},{7,6},{5,7},{3,5},{1,3},{0,1},{10,8},{12,10},{14... | collective-permute-start | bytes 1179656 | tf_op jit(solution)/shard_map/ppermute | solution.py:498
  11.4 15.9 %collective-permute-start.4 = (bf16[64,3072]{1,0:T(8,128)(2,1)}, bf16[64,3072]{1,0:T(8,128)(2,1)S(1)}, u32[]{:S(2)}, u32[]{:S(2)}) collective-permute-start(bf16[64,3072]{1,0:T(8,128)(2,1)} %refs_4_.7), channel_id=1, source_target_pairs={{0,2},{2,4},{4,6},{6,7},{7,5},{5,3},{3,1},{1,0},{8,10},{10,12},{12... | collective-permute-start | bytes 1179656 | tf_op jit(solution)/shard_map/ppermute | solution.py:494
  27.3 10.2 %copy-start.3 = (bf16[64,3072]{1,0:T(8,128)(2,1)}, bf16[64,3072]{1,0:T(8,128)(2,1)S(1)}, u32[]{:S(2)}) copy-start(bf16[64,3072]{1,0:T(8,128)(2,1)S(1)} %collective-permute-done.4.refs_1_.refs_3_) | copy-start | bytes 1179652
  27.3 21.2 %collective-permute-start.6 = (bf16[64,3072]{1,0:T(8,128)(2,1)S(1)}, bf16[64,3072]{1,0:T(8,128)(2,1)S(1)}, u32[]{:S(2)}, u32[]{:S(2)}) collective-permute-start(bf16[64,3072]{1,0:T(8,128)(2,1)S(1)} %collective-permute-done.4.refs_1_.refs_3_), channel_id=1, source_target_pairs={{0,2},{2,4},{4,6},{6,7},{7,5},{5,3},{3,1},{1,0},{8,10},{10,12},{12... | collective-permute-start | bytes 1179656 | tf_op jit(solution)/shard_map/ppermute | solution.py:494
  31.6 28.2 %copy-start.9 = (f32[3,200,128]{2,1,0:T(8,128)}, f32[3,200,128]{2,1,0:T(8,128)S(1)}, u32[]{:S(2)}) copy-start(f32[3,200,128]{2,1,0:T(8,128)S(1)} %get-tuple-element.52.mid_ref) | copy-start | bytes 921604
  31.6 18.7 %collective-permute-start.3 = (f32[3,200,128]{2,1,0:T(8,128)S(1)}, f32[3,200,128]{2,1,0:T(8,128)S(1)}, u32[]{:S(2)}, u32[]{:S(2)}) collective-permute-start(f32[3,200,128]{2,1,0:T(8,128)S(1)} %get-tuple-element.52.mid_ref), channel_id=1, source_target_pairs={{1,0},{2,1},{3,2},{4,3},{5,4},{6,5},{7,6},{9,8},{10,9},{11,10},{12... | collective-permute-start | bytes 921608 | tf_op jit(solution)/shard_map/ppermute | solution.py:29
  32.9 17.4 %collective-permute-start.2 = (f32[3,200,128]{2,1,0:T(8,128)S(1)}, f32[3,200,128]{2,1,0:T(8,128)S(1)}, u32[]{:S(2)}, u32[]{:S(2)}) collective-permute-start(f32[3,200,128]{2,1,0:T(8,128)S(1)} %get-tuple-element.52.mid_ref), channel_id=1, source_target_pairs={{0,1},{1,2},{2,3},{3,4},{4,5},{5,6},{6,7},{8,9},{9,10},{10,11},{11... | collective-permute-start | bytes 921608 | tf_op jit(solution)/shard_map/ppermute | solution.py:29
  37.4 0.8 copy-start.2
  47.5 10.9 %collective-permute-start.7 = (bf16[64,3072]{1,0:T(8,128)(2,1)}, bf16[64,3072]{1,0:T(8,128)(2,1)S(1)}, u32[]{:S(2)}, u32[]{:S(2)}) collective-permute-start(bf16[64,3072]{1,0:T(8,128)(2,1)} %copy-done.2), channel_id=1, source_target_pairs={{2,0},{4,2},{6,4},{7,6},{5,7},{3,5},{1,3},{0,1},{10,8},{12,10},{14... | collective-permute-start | bytes 1179656 | tf_op jit(solution)/shard_map/ppermute | solution.py:498
  48.5 28.3 %copy-start = (bf16[64,3072]{1,0:T(8,128)(2,1)}, bf16[64,3072]{1,0:T(8,128)(2,1)S(1)}, u32[]{:S(2)}) copy-start(bf16[64,3072]{1,0:T(8,128)(2,1)S(1)} %collective-permute-done.6.refs_0_.refs_2_) | copy-start | bytes 1179652
  48.5 11.3 %collective-permute-start.8 = (bf16[64,3072]{1,0:T(8,128)(2,1)S(1)}, bf16[64,3072]{1,0:T(8,128)(2,1)S(1)}, u32[]{:S(2)}, u32[]{:S(2)}) collective-permute-start(bf16[64,3072]{1,0:T(8,128)(2,1)S(1)} %collective-permute-done.6.refs_0_.refs_2_), channel_id=1, source_target_pairs={{0,2},{2,4},{4,6},{6,7},{7,5},{5,3},{3,1},{1,0},{8,10},{10,12},{12... | collective-permute-start | bytes 1179656 | tf_op jit(solution)/shard_map/ppermute | solution.py:494
  50.2 34.7 %copy-start.7 = (f32[3,200,128]{2,1,0:T(8,128)}, f32[3,200,128]{2,1,0:T(8,128)S(1)}, u32[]{:S(2)}) copy-start(f32[3,200,128]{2,1,0:T(8,128)S(1)} %collective-permute-done.3.high_ref) | copy-start | bytes 921604
  50.2 34.7 %copy-start.8 = (f32[3,200,128]{2,1,0:T(8,128)}, f32[3,200,128]{2,1,0:T(8,128)S(1)}, u32[]{:S(2)}) copy-start(f32[3,200,128]{2,1,0:T(8,128)S(1)} %collective-permute-done.2.low_ref) | copy-start | bytes 921604
  58.4 18.4 %copy-start.1 = (bf16[64,3072]{1,0:T(8,128)(2,1)}, bf16[64,3072]{1,0:T(8,128)(2,1)S(1)}, u32[]{:S(2)}) copy-start(bf16[64,3072]{1,0:T(8,128)(2,1)S(1)} %collective-permute-done.7.refs_1_.refs_6_) | copy-start | bytes 1179652
  58.4 27.3 %collective-permute-start.9 = (bf16[64,3072]{1,0:T(8,128)(2,1)S(1)}, bf16[64,3072]{1,0:T(8,128)(2,1)S(1)}, u32[]{:S(2)}, u32[]{:S(2)}) collective-permute-start(bf16[64,3072]{1,0:T(8,128)(2,1)S(1)} %collective-permute-done.7.refs_1_.refs_6_), channel_id=1, source_target_pairs={{2,0},{4,2},{6,4},{7,6},{5,7},{3,5},{1,3},{0,1},{10,8},{12,10},{14... | collective-permute-start | bytes 1179656 | tf_op jit(solution)/shard_map/ppermute | solution.py:498
  59.8 25.1 %copy-start.4 = (bf16[64,3072]{1,0:T(8,128)(2,1)}, bf16[64,3072]{1,0:T(8,128)(2,1)S(1)}, u32[]{:S(2)}) copy-start(bf16[64,3072]{1,0:T(8,128)(2,1)S(1)} %collective-permute-done.8.refs_0_.refs_1_) | copy-start | bytes 1179652
  59.8 26.0 %collective-permute-start.10 = (bf16[64,3072]{1,0:T(8,128)(2,1)S(1)}, bf16[64,3072]{1,0:T(8,128)(2,1)S(1)}, u32[]{:S(2)}, u32[]{:S(2)}) collective-permute-start(bf16[64,3072]{1,0:T(8,128)(2,1)S(1)} %collective-permute-done.8.refs_0_.refs_1_), channel_id=1, source_target_pairs={{0,2},{2,4},{4,6},{6,7},{7,5},{5,3},{3,1},{1,0},{8,10},{10,12},{12... | collective-permute-start | bytes 1179656 | tf_op jit(solution)/shard_map/ppermute | solution.py:494
  76.8 20.6 %copy-start.21 = (f32[3,256]{1,0:T(4,128)S(1)}, f32[3,256]{1,0:T(4,128)}, u32[]{:S(2)}) copy-start(f32[3,256]{1,0:T(4,128)} %context_field.3) | copy-start | bytes 9220
  84.9 12.4 %copy-start.22 = (f32[3,128]{1,0:T(4,128)S(1)}, f32[3,128]{1,0:T(4,128)}, u32[]{:S(2)}) copy-start(f32[3,128]{1,0:T(4,128)} %context_field.4) | copy-start | bytes 4612
  85.8 0.7 copy-start.5
  85.8 0.9 copy-start.6
  99.1 12.2 %all-to-all-start = ((f32[32,1,1536]{2,1,0:T(1,128)}), f32[32,1,1536]{2,1,0:T(1,128)S(1)}, u32[]{:S(2)}, u32[]{:S(2)}) async-start(f32[32,1,1536]{2,1,0:T(1,128)} %reshape.200), calls=%async_computation | async-start | bytes 393216 | tf_op jit(solution)/shard_map/all_to_all | solution.py:520
  126.8 4.3 %collective-permute-start.12 = (f32[96,128]{1,0:T(8,128)}, f32[96,128]{1,0:T(8,128)S(1)}, u32[]{:S(2)}, u32[]{:S(2)}) collective-permute-start(f32[96,128]{1,0:T(8,128)} %get-tuple-element.31), channel_id=1, source_target_pairs={{8,0},{16,8},{24,16},{9,1},{17,9},{25,17},{10,2},{18,10},{26,18},{... | collective-permute-start | bytes 147464 | tf_op jit(solution)/shard_map/ppermute | solution.py:29
  128.1 4.1 %collective-permute-start.11 = (f32[96,128]{1,0:T(8,128)}, f32[96,128]{1,0:T(8,128)S(1)}, u32[]{:S(2)}, u32[]{:S(2)}) collective-permute-start(f32[96,128]{1,0:T(8,128)} %get-tuple-element.31), channel_id=1, source_target_pairs={{0,8},{8,16},{16,24},{1,9},{9,17},{17,25},{2,10},{10,18},{18,26},{... | collective-permute-start | bytes 147464 | tf_op jit(solution)/shard_map/ppermute | solution.py:29
  133.0 12.1 %copy-start.12 = (f32[3,96,128]{2,1,0:T(8,128)}, f32[3,96,128]{2,1,0:T(8,128)S(1)}, u32[]{:S(2)}) copy-start(f32[3,96,128]{2,1,0:T(8,128)S(1)} %pad_maximum_fusion.3.mid_ref) | copy-start | bytes 442372
  133.1 7.5 %collective-permute-start.14 = (f32[3,96,128]{2,1,0:T(8,128)S(1)}, f32[3,96,128]{2,1,0:T(8,128)S(1)}, u32[]{:S(2)}, u32[]{:S(2)}) collective-permute-start(f32[3,96,128]{2,1,0:T(8,128)S(1)} %pad_maximum_fusion.3.mid_ref), channel_id=1, source_target_pairs={{1,0},{2,1},{3,2},{4,3},{5,4},{6,5},{7,6},{9,8},{10,9},{11,10},{12... | collective-permute-start | bytes 442376 | tf_op jit(solution)/shard_map/ppermute | solution.py:29
  134.4 10.8 %collective-permute-start.13 = (f32[3,96,128]{2,1,0:T(8,128)S(1)}, f32[3,96,128]{2,1,0:T(8,128)S(1)}, u32[]{:S(2)}, u32[]{:S(2)}) collective-permute-start(f32[3,96,128]{2,1,0:T(8,128)S(1)} %pad_maximum_fusion.3.mid_ref), channel_id=1, source_target_pairs={{0,1},{1,2},{2,3},{3,4},{4,5},{5,6},{6,7},{8,9},{9,10},{10,11},{11... | collective-permute-start | bytes 442376 | tf_op jit(solution)/shard_map/ppermute | solution.py:29
  140.6 4.6 %copy-start.17 = (f32[3,96,128]{2,1,0:T(8,128)}, f32[3,96,128]{2,1,0:T(8,128)S(1)}, u32[]{:S(2)}) copy-start(f32[3,96,128]{2,1,0:T(8,128)S(1)} %collective-permute-done.14.high_ref) | copy-start | bytes 442372
  145.2 0.7 copy-start.19
  156.2 4.3 %collective-permute-start.16 = (f32[96,128]{1,0:T(8,128)}, f32[96,128]{1,0:T(8,128)S(1)}, u32[]{:S(2)}, u32[]{:S(2)}) collective-permute-start(f32[96,128]{1,0:T(8,128)} %sweep.5), channel_id=1, source_target_pairs={{8,0},{16,8},{24,16},{9,1},{17,9},{25,17},{10,2},{18,10},{26,18},{... | collective-permute-start | bytes 147464 | tf_op jit(solution)/shard_map/ppermute | solution.py:29
  157.5 4.1 %collective-permute-start.15 = (f32[96,128]{1,0:T(8,128)}, f32[96,128]{1,0:T(8,128)S(1)}, u32[]{:S(2)}, u32[]{:S(2)}) collective-permute-start(f32[96,128]{1,0:T(8,128)} %sweep.5), channel_id=1, source_target_pairs={{0,8},{8,16},{16,24},{1,9},{9,17},{17,25},{2,10},{10,18},{18,26},{... | collective-permute-start | bytes 147464 | tf_op jit(solution)/shard_map/ppermute | solution.py:29
  162.4 12.8 %copy-start.13 = (f32[3,96,128]{2,1,0:T(8,128)}, f32[3,96,128]{2,1,0:T(8,128)S(1)}, u32[]{:S(2)}) copy-start(f32[3,96,128]{2,1,0:T(8,128)S(1)} %pad_maximum_fusion.4.mid_ref) | copy-start | bytes 442372
  162.4 66.5 %copy-start.14 = (f32[24,64]{1,0:T(8,128)S(1)}, f32[24,64]{1,0:T(8,128)}, u32[]{:S(2)}) copy-start(f32[24,64]{1,0:T(8,128)} %reduce_sum.19.field_ref) | copy-start | bytes 18436
  162.4 8.2 %collective-permute-start.18 = (f32[3,96,128]{2,1,0:T(8,128)S(1)}, f32[3,96,128]{2,1,0:T(8,128)S(1)}, u32[]{:S(2)}, u32[]{:S(2)}) collective-permute-start(f32[3,96,128]{2,1,0:T(8,128)S(1)} %pad_maximum_fusion.4.mid_ref), channel_id=1, source_target_pairs={{1,0},{2,1},{3,2},{4,3},{5,4},{6,5},{7,6},{9,8},{10,9},{11,10},{12... | collective-permute-start | bytes 442376 | tf_op jit(solution)/shard_map/ppermute | solution.py:29
  163.9 11.3 %collective-permute-start.17 = (f32[3,96,128]{2,1,0:T(8,128)S(1)}, f32[3,96,128]{2,1,0:T(8,128)S(1)}, u32[]{:S(2)}, u32[]{:S(2)}) collective-permute-start(f32[3,96,128]{2,1,0:T(8,128)S(1)} %pad_maximum_fusion.4.mid_ref), channel_id=1, source_target_pairs={{0,1},{1,2},{2,3},{3,4},{4,5},{5,6},{6,7},{8,9},{9,10},{10,11},{11... | collective-permute-start | bytes 442376 | tf_op jit(solution)/shard_map/ppermute | solution.py:29
  170.6 4.6 %copy-start.18 = (f32[3,96,128]{2,1,0:T(8,128)}, f32[3,96,128]{2,1,0:T(8,128)S(1)}, u32[]{:S(2)}) copy-start(f32[3,96,128]{2,1,0:T(8,128)S(1)} %collective-permute-done.18.high_ref) | copy-start | bytes 442372
  175.2 0.7 copy-start.20
  186.2 4.3 %collective-permute-start.20 = (f32[96,128]{1,0:T(8,128)}, f32[96,128]{1,0:T(8,128)S(1)}, u32[]{:S(2)}, u32[]{:S(2)}) collective-permute-start(f32[96,128]{1,0:T(8,128)} %sweep.6), channel_id=1, source_target_pairs={{8,0},{16,8},{24,16},{9,1},{17,9},{25,17},{10,2},{18,10},{26,18},{... | collective-permute-start | bytes 147464 | tf_op jit(solution)/shard_map/ppermute | solution.py:29
  187.5 4.1 %collective-permute-start.19 = (f32[96,128]{1,0:T(8,128)}, f32[96,128]{1,0:T(8,128)S(1)}, u32[]{:S(2)}, u32[]{:S(2)}) collective-permute-start(f32[96,128]{1,0:T(8,128)} %sweep.6), channel_id=1, source_target_pairs={{0,8},{8,16},{16,24},{1,9},{9,17},{17,25},{2,10},{10,18},{18,26},{... | collective-permute-start | bytes 147464 | tf_op jit(solution)/shard_map/ppermute | solution.py:29
  192.5 12.6 %copy-start.11 = (f32[3,96,128]{2,1,0:T(8,128)}, f32[3,96,128]{2,1,0:T(8,128)S(1)}, u32[]{:S(2)}) copy-start(f32[3,96,128]{2,1,0:T(8,128)S(1)} %pad_maximum_fusion.5.mid_ref) | copy-start | bytes 442372
  192.5 8.0 %collective-permute-start.22 = (f32[3,96,128]{2,1,0:T(8,128)S(1)}, f32[3,96,128]{2,1,0:T(8,128)S(1)}, u32[]{:S(2)}, u32[]{:S(2)}) collective-permute-start(f32[3,96,128]{2,1,0:T(8,128)S(1)} %pad_maximum_fusion.5.mid_ref), channel_id=1, source_target_pairs={{1,0},{2,1},{3,2},{4,3},{5,4},{6,5},{7,6},{9,8},{10,9},{11,10},{12... | collective-permute-start | bytes 442376 | tf_op jit(solution)/shard_map/ppermute | solution.py:29
  193.8 11.3 %collective-permute-start.21 = (f32[3,96,128]{2,1,0:T(8,128)S(1)}, f32[3,96,128]{2,1,0:T(8,128)S(1)}, u32[]{:S(2)}, u32[]{:S(2)}) collective-permute-start(f32[3,96,128]{2,1,0:T(8,128)S(1)} %pad_maximum_fusion.5.mid_ref), channel_id=1, source_target_pairs={{0,1},{1,2},{2,3},{3,4},{4,5},{5,6},{6,7},{8,9},{9,10},{10,11},{11... | collective-permute-start | bytes 442376 | tf_op jit(solution)/shard_map/ppermute | solution.py:29
  200.5 4.6 %copy-start.15 = (f32[3,96,128]{2,1,0:T(8,128)}, f32[3,96,128]{2,1,0:T(8,128)S(1)}, u32[]{:S(2)}) copy-start(f32[3,96,128]{2,1,0:T(8,128)S(1)} %collective-permute-done.22.high_ref) | copy-start | bytes 442372
  205.1 0.7 copy-start.16
  217.7 16.1 %all-to-all-start.1 = ((f32[32,16,128]{2,1,0:T(8,128)}), f32[32,16,128]{2,1,0:T(8,128)S(1)}, u32[]{:S(2)}, u32[]{:S(2)}) async-start(f32[32,16,128]{2,1,0:T(8,128)} %broadcast_in_dim.50), calls=%async_computation.1 | async-start | bytes 524288 | tf_op jit(solution)/shard_map/all_to_all | solution.py:554
  233.9 0.7 copy-start.10

commit v2 on v0

v2 whole, which is shorter than its diff:
```python
import functools

import jax
import jax.numpy as jnp
from jax import lax
from jax.experimental import pallas as pl
from jax.experimental.pallas import tpu as pltpu
from jax.sharding import PartitionSpec as P


SWEEPS = 4
COUPLING = 2e-07
SOFTEN = 4e-05
BRICK = 0.1
SLAB = 0.03
REACH = 2
BOTH = ("grp", "dev")
F32 = jnp.float32
BF16 = jnp.bfloat16
TERMS = 16
PARTS = 2
VMEM = pl.BlockSpec(memory_space=pltpu.VMEM)
SMEM = pl.BlockSpec(memory_space=pltpu.SMEM)


def shift(block, axis, step):
    count = lax.axis_size(axis)
    pairs = [(i, i + step) for i in range(count) if 0 <= i + step < count]
    return lax.ppermute(block, axis, pairs)


def exchange(block):
    low, high = shift(block, "dev", 1), shift(block, "dev", -1)
    column = jnp.stack([low, block, high])
    low, high = shift(column, "grp", 1), shift(column, "grp", -1)
    return low, column, high


def limits(mib):
    return pltpu.CompilerParams(vmem_limit_bytes=mib << 20)


def whole(array):
    return pl.BlockSpec(array.shape, lambda *_: (0,) * len(array.shape))


def ring_order(count):
    return list(range(0, count, 2)) + [i for i in range(count - 1, 0, -1) if i % 2]


def source_of(at_ref, offset, count):
    dev = at_ref[1]
    half = lax.div(dev, 2)
    place = jnp.where(lax.rem(dev, 2) == 0, half, count - 1 - half)
    place = lax.rem(place + offset + count, count)
    return jnp.where(place < (count + 1) // 2, 2 * place, 2 * (count - 1 - place) + 1)


def split(value):
    high = value.astype(BF16).astype(F32)
    rest = value - high
    middle = rest.astype(BF16).astype(F32)
    return high, middle, rest - middle


def weights_kernel(
    per_step, blocks, at_ref, links_ref, low_ref, mid_ref, high_ref, out_ref, coords_ref, far_ref, own_ref, side_ref
):
    width = out_ref.shape[2]
    listed = out_ref.shape[1] // width
    middle_x = (at_ref[0].astype(F32) + 0.5) * BRICK
    middle_y = (at_ref[1].astype(F32) + 0.5) * BRICK
    level = lax.broadcasted_iota(jnp.int32, (blocks, width), 0).astype(F32)
    middle_z = (level + 0.5) * SLAB

    def pieces(x, y, z, more):
        coords = [split(value) for value in (x, y, z)]
        norm = split(x * x + y * y + z * z + more)
        return [c[part] for part in range(3) for c in coords] + list(norm)

    for a, ref in enumerate((low_ref, mid_ref, high_ref)):

        def fill(b, carry, a=a, ref=ref):
            rows = pl.ds(pl.multiple_of((3 * a + b) * blocks, blocks), blocks)
            x = ref[b, :blocks, :] - middle_x
            y = ref[b, blocks : 2 * blocks, :] - middle_y
            z = ref[b, 2 * blocks : 3 * blocks, :] - middle_z
            for k, value in enumerate((x, y, z)):
                coords_ref[k, rows, :] = value
            for at, value in enumerate(pieces(x, y, z, 0.0)):
                far_ref[rows, at, :] = value
            return carry

        lax.fori_loop(0, 3, fill, 0)
    base = slice(4 * blocks, 5 * blocks)
    x, y, middle = coords_ref[0, base, :], coords_ref[1, base, :], coords_ref[2, base, :]

    def own(hop, carry):
        z = middle - (hop - REACH).astype(F32) * SLAB
        for at, value in enumerate(pieces(x, y, z, SOFTEN)):
            own_ref[hop, :, at, :] = value
        return carry

    lax.fori_loop(0, 2 * REACH + 1, own, 0)
    diagonal = lax.broadcasted_iota(jnp.int32, (width, width), 0) == lax.broadcasted_iota(
        jnp.int32, (width, width), 1
    )
    row = lax.broadcasted_iota(jnp.int32, (8, width), 0)
    ones = jnp.ones((3, width), F32)

    def some(step, carry):
        for inner in range(per_step):
            block = step * per_step + inner
            for hop in range(2 * REACH + 1):
                high = -2.0 * own_ref[hop, block, 0:3, :]
                mid = -2.0 * own_ref[hop, block, 3:6, :]
                low = -2.0 * own_ref[hop, block, 6:9, :]
                norm = own_ref[hop, block, 9:12, :]
                none = jnp.zeros((3, width), F32)
                side = jnp.concatenate(
                    [high, high, high, ones, norm, none[:1], mid, mid, none[:2], low, none, none[:2]], axis=0
                )
                side_ref[inner, hop] = side.astype(BF16)
        for inner in range(per_step):
            block = step * per_step + inner
            for n in range(listed):
                link = links_ref[block, n]
                hop = lax.rem(link, blocks) - block + REACH
                top = far_ref[link, 0:8, :]
                end = far_ref[link, 8:16, :]
                end = jnp.where(row < 4, end, jnp.where(row < 7, 1.0, 0.0))
                square = lax.dot_general(
                    jnp.concatenate([top, end, top, top], axis=0).astype(BF16),
                    side_ref[inner, hop],
                    (((0,), (0,)), ((), ())),
                    preferred_element_type=F32,
                )
                root = lax.rsqrt(square)
                two = root * root
                value = two * two * root
                if n == 0:
                    value = jnp.where(diagonal, 0.0, value)
                out_ref[block, n * width : (n + 1) * width, :] = value.astype(BF16)
        return carry

    lax.fori_loop(0, blocks // per_step, some, 0)


def pair_weights(at, links, around, blocks):
    listed = links.shape[1]
    width = around[0].shape[2]
    region = 9 * blocks
    coords = jax.ShapeDtypeStruct((3, region, width), F32)
    return pl.pallas_call(
        functools.partial(weights_kernel, 4, blocks),
        out_shape=[jax.ShapeDtypeStruct((blocks, listed * width, width), BF16), coords],
        in_specs=[SMEM, SMEM] + [VMEM] * 3,
        out_specs=[VMEM, VMEM],
        scratch_shapes=[
            pltpu.VMEM((region, 24, width), F32),
            pltpu.VMEM((2 * REACH + 1, blocks, 24, width), F32),
            pltpu.VMEM((4, 2 * REACH + 1, 32, width), BF16),
        ],
        compiler_params=limits(12),
        name="pair_weights",
    )(at, links, *around)


def sweep_kernel(per_step, blocks, first, last, base, at_ref, links_ref, *refs):
    refs = list(refs)
    if first:
        spot_ref, polar_ref, parts_ref = refs.pop(0), refs.pop(0), refs.pop(0)
    if last:
        target_ref = refs.pop(0)
    coords_ref, low_ref, mid_ref, high_ref, weights_ref, alpha_ref, total_ref, out_ref = refs[:8]
    refs = refs[8:]
    if first:
        sum_ref, field_ref = refs.pop(0), refs.pop(0)
    if last:
        pick_ref = refs.pop(0)
    v_ref, w_ref, p_ref = refs[:3]
    _, width = coords_ref.shape[1:]
    listed = weights_ref.shape[1] // width
    own_base = 4 * blocks
    lane = lax.broadcasted_iota(jnp.int32, (1, width), 1)

    if first:
        scalar_ref, sem = refs[3:]
        parts = parts_ref.shape[0]
        field = parts_ref[0]
        for i in range(1, parts):
            field = field + parts_ref[i]
        field_ref[...] = field
        copy = pltpu.make_async_copy(field_ref, scalar_ref, sem)
        copy.start()
    for a, ref in enumerate((low_ref, mid_ref, high_ref)):
        for b in range(3):
            for k in range(3):
                v_ref[k, (3 * a + b) * blocks : (3 * a + b + 1) * blocks, :] = ref[
                    b, base + k * blocks : base + (k + 1) * blocks, :
                ]
    if first:
        sum_ref[...] = total_ref[...]
        copy.wait()
        groups, members, per_brick = at_ref[2], at_ref[3], at_ref[4]
        lines = field_ref.shape[0] // 3

        def place(p, grp, dev, own):
            t = (grp * members + dev) * per_brick
            line, start = t // width, t % width

            def one(j, carry):
                here = lane == spot_ref[1, p, j]
                row = spot_ref[0, p, j]
                for k in range(3):
                    value = scalar_ref[k * lines + line, start + j]
                    if own:
                        sum_ref[pl.ds(k * blocks + row, 1), :] += jnp.where(here, value, 0.0)
                    else:
                        add = jnp.where(here, value * polar_ref[p, j], 0.0)
                        v_ref[k, pl.ds(p * blocks + row, 1), :] += add
                return carry

            lax.fori_loop(0, spot_ref.shape[2], one, 0, unroll=8)

        def brick(p, carry):
            grp = jnp.clip(at_ref[0] + p // 3 - 1, 0, groups - 1)
            dev = jnp.clip(at_ref[1] + p % 3 - 1, 0, members - 1)
            place(p, grp, dev, False)
            return carry

        lax.fori_loop(0, 9, brick, 0)
        place(4, at_ref[0], at_ref[1], True)

    row = lax.broadcasted_iota(jnp.int32, (TERMS, width), 0)
    which = lax.rem(row, 3)

    def some(step, carry):
        for inner in range(per_step):
            block = step * per_step + inner
            for n in range(listed):
                link = links_ref[block, n]
                away = (lax.rem(link, blocks) - block).astype(F32) * SLAB
                x = coords_ref[0, pl.ds(link, 1), :]
                y = coords_ref[1, pl.ds(link, 1), :]
                z = coords_ref[2, pl.ds(link, 1), :] + away
                v0, v1, v2 = (v_ref[k, pl.ds(link, 1), :] for k in range(3))
                along = x * v0 + y * v1 + z * v2
                third = (x * x + y * y + z * z) * (1.0 / 3.0)
                dipole = jnp.where(which == 0, v0, jnp.where(which == 1, v1, v2))
                spot = jnp.where(
                    row < 3,
                    1.0,
                    jnp.where(
                        (row < 6) | (row == 12), x, jnp.where((row < 9) | (row == 13), y, z)
                    ),
                )
                value = jnp.where(row < 12, spot * dipole, spot * along - third * dipole)
                cols = slice(n * width, (n + 1) * width)
                for part in range(PARTS):
                    piece = value.astype(BF16)
                    w_ref[inner, part * TERMS : (part + 1) * TERMS, cols] = piece
                    if part < PARTS - 1:
                        value = value - piece.astype(F32)
            product = jnp.dot(w_ref[inner], weights_ref[block], preferred_element_type=F32)
            total = product[:TERMS]
            for part in range(1, PARTS):
                total = total + product[part * TERMS : (part + 1) * TERMS]
            p_ref[block] = total
        return carry

    lax.fori_loop(0, blocks // per_step, some, 0)
    x = [coords_ref[k, own_base : own_base + blocks, :] for k in range(3)]
    term = [p_ref[:, r, :] for r in range(15)]
    p = term[:3]
    m = [term[3 + 3 * k : 6 + 3 * k] for k in range(3)]
    q = term[12:15]
    inside = x[0] * p[0] + x[1] * p[1] + x[2] * p[2] - (m[0][0] + m[1][1] + m[2][2])
    size = x[0] * x[0] + x[1] * x[1] + x[2] * x[2] + SOFTEN
    alpha = alpha_ref[...]
    for k in range(3):
        one = x[0] * m[k][0] + x[1] * m[k][1] + x[2] * m[k][2]
        other = x[0] * m[0][k] + x[1] * m[1][k] + x[2] * m[2][k]
        force = x[k] * inside - one + q[k] - (size * p[k] - 2.0 * other) * (1.0 / 3.0)
        rows = slice(k * blocks, (k + 1) * blocks)
        given = sum_ref[rows, :] if first else total_ref[rows, :]
        out_ref[rows, :] = alpha * (given + (3.0 * COUPLING) * force)
    if last:
        per_brick = target_ref.shape[0]
        for j in range(per_brick):
            site = target_ref[j]
            here = lane == site % width
            line = jnp.zeros((1, width), F32)
            for k in range(3):
                values = out_ref[pl.ds(k * blocks + site // width, 1), :]
                found = jnp.sum(jnp.where(here, values, 0.0), axis=1, keepdims=True)
                line = jnp.where(lane == k, found, line)
            pick_ref[0, j : j + 1, :] = line
        for i in range(1, pick_ref.shape[0]):
            pick_ref[i] = pick_ref[0]


def sweep(at, links, coords, around, weights, alpha, total, tail=None, parts=None, target=None, copies=1):
    blocks, depth, width = weights.shape
    region = coords.shape[1]
    first, last = parts is not None, target is not None
    per_step = 8
    rows = jax.ShapeDtypeStruct((3 * blocks, width), F32)
    outs = [rows]
    scratch = [
        pltpu.VMEM((3, region, width), F32),
        pltpu.VMEM((per_step, PARTS * TERMS, depth), BF16),
        pltpu.VMEM((blocks, TERMS, width), F32),
    ]
    given, specs = [at, links], [SMEM, SMEM]
    if first:
        outs += [rows, jax.ShapeDtypeStruct(parts.shape[1:], F32)]
        given += [*tail, parts]
        specs += [SMEM, SMEM, VMEM]
        scratch += [pltpu.SMEM(parts.shape[1:], F32), pltpu.SemaphoreType.DMA]
    if last:
        outs.append(jax.ShapeDtypeStruct((copies, target.shape[0], width), F32))
        given.append(target)
        specs.append(SMEM)
    return pl.pallas_call(
        functools.partial(sweep_kernel, per_step, blocks, first, last, 3 * blocks if first else 0),
        out_shape=outs,
        in_specs=specs + [VMEM] * 7,
        out_specs=[VMEM] * len(outs),
        scratch_shapes=scratch,
        compiler_params=limits(8),
        name="sweep",
    )(*given, coords, *around, weights, alpha, total)


def context_kernel(count, offsets, members, more, at_ref, *refs):
    lefts = refs[:count]
    density_ref = refs[count]
    rights = refs[count + 1 : 2 * count + 1]
    refs = refs[2 * count + 1 :]
    before_ref = refs[0] if more else None
    directions_ref, out_ref, flip_ref, left_ref, sums_ref = refs[-5:]
    step = pl.program_id(0)
    rows = lefts[0].shape[0]

    @pl.when(step == 0)
    def _():
        for i, ref in enumerate(lefts):
            left_ref[i * rows : (i + 1) * rows, :] = ref[...]
        sums_ref[...] = jnp.zeros_like(sums_ref)

    cut = flip_ref.shape[0]
    begin = pl.multiple_of(step * cut, cut)
    flip_ref[...] = jnp.transpose(left_ref[:, pl.ds(begin, cut)])
    context = jnp.dot(left_ref[...], density_ref[...], preferred_element_type=F32)
    lanes = context.shape[1]
    for i, ref in enumerate(rights):
        weighted = context[i * rows : (i + 1) * rows] * ref[...].astype(F32)
        for k in range(3):
            term = weighted * directions_ref[k : k + 1, :]
            folded = term[:, :128]
            for at in range(128, lanes, 128):
                folded = folded + term[:, at : at + 128]
            sums_ref[k, i * rows : (i + 1) * rows, :] += folded

    @pl.when(step == pl.num_programs(0) - 1)
    def _():
        lines = members * rows // 128
        per_line = 128 // rows
        slot = lax.broadcasted_iota(jnp.int32, (1, 128), 1) // rows
        if more:
            out_ref[0] = before_ref[0]
        else:
            out_ref[0] = jnp.zeros_like(out_ref[0])
        for k in range(3):
            for pair in range(sums_ref.shape[1] // 128):
                flipped = jnp.transpose(sums_ref[k, pair * 128 : (pair + 1) * 128, :])
                line = jnp.sum(flipped, axis=0, keepdims=True)
                for inside in range(per_line):
                    i = pair * per_line + inside
                    if i >= count:
                        continue
                    source = source_of(at_ref, offsets[i], members)
                    spread = line
                    for turn in range(1, per_line):
                        spread = jnp.where(
                            slot == (inside + turn) % per_line, pltpu.roll(line, turn * rows, 1), spread
                        )
                    row = k * lines + source // per_line
                    old = out_ref[0, pl.ds(row, 1), :]
                    out_ref[0, pl.ds(row, 1), :] = jnp.where(slot == source % per_line, spread, old)
        for i in range(1, out_ref.shape[0]):
            out_ref[i] = out_ref[0]


def context_field(at, offsets, members, chunks, density, right, directions, before, copies):
    count = len(chunks)
    rows, depth = chunks[0].shape
    columns = density.shape[1]
    tile = 256
    padded = -(-count * rows // 128) * 128
    lines = members * rows // 128
    more = before is not None

    def right_block(offset):
        return pl.BlockSpec((rows, tile), lambda j, at_ref: (source_of(at_ref, offset, members), j))

    out = jax.ShapeDtypeStruct((copies, 3 * lines, 128), F32)
    return pl.pallas_call(
        functools.partial(context_kernel, count, offsets, members, more),
        out_shape=[out, jax.ShapeDtypeStruct((depth, count * rows), BF16)],
        grid_spec=pltpu.PrefetchScalarGridSpec(
            num_scalar_prefetch=1,
            grid=(columns // tile,),
            in_specs=[whole(c) for c in chunks]
            + [pl.BlockSpec((depth, tile), lambda j, at_ref: (0, j))]
            + [right_block(o) for o in offsets]
            + ([whole(before)] if more else [])
            + [pl.BlockSpec((3, tile), lambda j, at_ref: (0, j))],
            out_specs=[
                whole(out),
                pl.BlockSpec((depth * tile // columns, count * rows), lambda j, at_ref: (j, 0)),
            ],
            scratch_shapes=[
                pltpu.VMEM((count * rows, depth), BF16),
                pltpu.VMEM((3, padded, 128), F32),
            ],
        ),
        compiler_params=limits(20),
        name="context_field",
    )(at, *chunks, density, *([right] * count), *([before] if more else []), directions)


def fock_kernel(groups, members, at_ref, *refs):
    count = len(groups)
    lefts = refs[:count]
    right_ref, directions_ref, dipoles_ref, out_ref, scaled_ref = refs[count:]
    rows = right_ref.shape[0] // members

    @pl.when(pl.program_id(0) == 0)
    def _():
        lines = [directions_ref[k : k + 1, :] for k in range(3)]
        for i, offset in enumerate(sum(groups, [])):
            start = pl.multiple_of(source_of(at_ref, offset, members) * rows, rows)
            dipoles = dipoles_ref[pl.ds(start, rows), :]
            along = dipoles[:, 0:1] * lines[0]
            for k in (1, 2):
                along = along + dipoles[:, k : k + 1] * lines[k]
            value = right_ref[pl.ds(start, rows), :].astype(F32) * along
            scaled_ref[i * rows : (i + 1) * rows, :] = (-value).astype(BF16)

    left = jnp.concatenate([ref[...] for ref in lefts], axis=1)
    out_ref[...] = jnp.dot(left, scaled_ref[...], preferred_element_type=F32)


def fock_term(at, groups, members, lefts, right, directions, dipoles):
    depth = lefts[0].shape[0]
    targets, columns = right.shape
    tile = 512
    return pl.pallas_call(
        functools.partial(fock_kernel, groups, members),
        out_shape=jax.ShapeDtypeStruct((depth, columns), F32),
        grid_spec=pltpu.PrefetchScalarGridSpec(
            num_scalar_prefetch=1,
            grid=(depth // tile,),
            in_specs=[pl.BlockSpec((tile, a.shape[1]), lambda i, at_ref: (i, 0)) for a in lefts]
            + [whole(right), whole(directions), whole(dipoles)],
            out_specs=pl.BlockSpec((tile, columns), lambda i, at_ref: (i, 0)),
            scratch_shapes=[pltpu.VMEM((targets, columns), BF16)],
        ),
        name="fock_term",
    )(at, *lefts, right, directions, dipoles)


def on_device(
    density, left_factor, right_factor, directions, places, alpha, static_field, neighbours, targets
):
    groups = lax.axis_size("grp")
    members = lax.axis_size("dev")
    grp = lax.axis_index("grp")
    dev = lax.axis_index("dev")
    rows = left_factor.shape[0]
    per_brick = targets.shape[2]
    sites = places.shape[3]
    blocks = neighbours.shape[2]
    width = sites // blocks
    devices = groups * members
    at = jnp.stack([grp, dev, jnp.int32(groups), jnp.int32(members), jnp.int32(per_brick)]).astype(jnp.int32)

    order = ring_order(members)
    forward = [(order[i], order[(i + 1) % members]) for i in range(members)]
    backward = [(b, a) for a, b in forward]
    chunks = {0: left_factor}
    onward = back = left_factor
    arrivals = [0]
    for step in range(1, members // 2 + 1):
        onward = lax.ppermute(onward, "dev", forward)
        chunks[-step] = onward
        arrivals.append(-step)
        if step <= (members - 1) // 2:
            back = lax.ppermute(back, "dev", backward)
            chunks[step] = back
            arrivals.append(step)

    links = neighbours[0, 0]
    polar = alpha[0, 0]
    own_targets = targets[0, 0]
    fixed = static_field[:, 0, 0]
    picked = jnp.sum(
        jnp.where(own_targets[:, None] == jnp.arange(sites, dtype=jnp.int32)[None, :], polar[None, :], 0.0),
        axis=1,
    )
    tail = jnp.pad(jnp.stack([own_targets.astype(F32), picked]), ((0, 6), (0, width - per_brick)))
    packed = jnp.concatenate(
        [
            places[:, 0, 0].reshape(3 * blocks, width),
            (polar[None] * fixed).reshape(3 * blocks, width),
            tail,
        ]
    )
    around = exchange(packed)
    tails = jnp.stack([a[:, 6 * blocks : 6 * blocks + 2, :per_brick] for a in around])
    tails = tails.reshape(9, 2, per_brick)
    sites_of = tails[:, 0].astype(jnp.int32)
    spots = jnp.stack([sites_of // width, sites_of % width])
    weights, coords = pair_weights(at, links, around, blocks)

    parts_of = [arrivals[i : i + 4] for i in range(0, len(arrivals), 4)]
    parts = None
    lefts = []
    for i, offsets in enumerate(parts_of):
        parts, left = context_field(
            at,
            offsets,
            members,
            [chunks[o] for o in offsets],
            density,
            right_factor,
            directions,
            parts,
            devices if i == len(parts_of) - 1 else 1,
        )
        lefts.append(left)
    parts = lax.all_to_all(parts, BOTH, 0, 0)

    alpha_rows = polar.reshape(blocks, width)
    total = fixed.reshape(3 * blocks, width)
    current, total, field = sweep(
        at, links, coords, around, weights, alpha_rows, total, tail=(spots, tails[:, 1]), parts=parts
    )
    for repeat in range(1, SWEEPS):
        around = exchange(current)
        if repeat < SWEEPS - 1:
            current = sweep(at, links, coords, around, weights, alpha_rows, total)[0]
        else:
            current, picks = sweep(
                at, links, coords, around, weights, alpha_rows, total, target=own_targets, copies=devices
            )
    dipoles = lax.all_to_all(picks, BOTH, 0, 0).reshape(devices * per_brick, width)
    fock_polar = fock_term(at, parts_of, members, lefts, right_factor, directions, dipoles)
    owner = grp * members + dev
    qm_local = lax.dynamic_slice_in_dim(field.reshape(3, members * rows), owner * per_brick, per_brick, 1)
    return (current.reshape(3, 1, 1, sites), qm_local, fock_polar)


def solution(mesh):
    placed = (
        P("grp", "dev"),
        P("dev", "grp"),
        P(None, "dev"),
        P(None, "dev"),
        P(None, "grp", "dev", None),
        P("grp", "dev", None),
        P(None, "grp", "dev", None),
        P("grp", "dev", None, None),
        P("grp", "dev", None),
    )
    return jax.shard_map(
        on_device,
        mesh=mesh,
        in_specs=placed,
        out_specs=(P(None, "grp", "dev", None), P(None, ("grp", "dev")), P("grp", "dev")),
        check_vma=False,
    )
```

time: 551 us -> 194 us (0.35)
  other arithmetic: 186 us -> 3.31 us
  blocking collectives: 107 us -> 0 us
  waiting for transfers between devices: 89.9 us -> 28.8 us
  Pallas kernels: 0 us -> 59.3 us
  local copies, waits for them, and re-layouts: 72.2 us -> 21.8 us
  starting transfers between devices: 52.1 us -> 78.6 us
  matrix products: 24.9 us -> 0 us
  between operations: 14.7 us -> 1.05 us
    reduce_sum x64 -> x1, other arithmetic: 152 us -> 0.93 us  [on_device(): jnp.sum(jnp.where(own_targets[:, None] == jnp.arange(sites, dtype=jnp.int...]
    all_gather x1 -> x0, blocking collectives: 66.1 us -> none  [on_device(): lax.all_gather(local_targets, ('grp', 'dev'), axis=1, tiled=True)]
    pallas_call x0 -> x8, Pallas kernels: none -> 59.3 us  [the longest x4 24.3 us: sweep(): pl.pallas_call(functools.partial(sweep_kernel, per_step, blocks, first, l...]
    all_gather x1 -> x0, waiting for transfers between devices: 56.4 us -> none  [on_device(): gathered = lax.all_gather(left_factor, 'dev', axis=0, tiled=True)]
    gather x128 -> x0, local copies, waits for them, and re-layouts: 41.1 us -> none  [the longest x64 20.6 us: one_group(): region_places[:, link_group].reshape(3, blocks_per_turn, listed * width)]
    unnamed x2 -> x0, blocking collectives: 41.1 us -> none
    mul x32 -> x1, other arithmetic: 30.1 us -> 0.81 us  [on_device(): polar[None] * fixed]
    dot_general x6 -> x0, matrix products: 24.9 us -> none  [the longest x1 9.63 us: on_device(): context = jnp.dot(gathered, density, preferred_element_type=jnp.float32)]
  transfers between devices with their start and end apart: 21 -> 25, of which waited for: 12 -> 14; matrix products, arithmetic and copies ran while one was open for 4% -> 2% of each run, Pallas kernels for 0% -> 8%
where the time goes in v2:
time: 194 us; the launch traced here: 193 us
  starting transfers between devices  78.6 us (41%)
  Pallas kernels  59.3 us (31%)
  waiting for transfers between devices  28.8 us (15%)
  local copies, waits for them, and re-layouts  21.8 us (11%)
  other arithmetic  3.31 us (2%)
    ppermute x16, starting transfers between devices, shift(): return lax.ppermute(block, axis, pairs)  46.5 us
    pallas_call x4, Pallas kernels, sweep(): pl.pallas_call(functools.partial(sweep_kernel, per_step, blocks, first, l...  24.3 us
    unnamed x36, local copies, waits for them, and re-layouts  21 us
    all_to_all x1, starting transfers between devices, on_device(): lax.all_to_all(picks, BOTH, 0, 0).reshape(devices * per_brick, width)  14.5 us
    pallas_call x2, Pallas kernels, context_field(): pl.pallas_call(functools.partial(context_kernel, count, offsets, members,...  13.7 us
    pallas_call x1, Pallas kernels, fock_term(): pl.pallas_call(functools.partial(fock_kernel, groups, members), out_shape...  12.7 us
    ppermute x16, waiting for transfers between devices, shift(): return lax.ppermute(block, axis, pairs)  9.92 us
    all_to_all x1, waiting for transfers between devices, on_device(): lax.all_to_all(picks, BOTH, 0, 0).reshape(devices * per_brick, width)  9.76 us
  transfers between devices with their start and end apart: 25, of which 14 were waited for; matrix products, arithmetic and copies ran while one was open for 2% of the time, Pallas kernels for 8%

profile of v2, /device:TPU:0, one launch (start us, length us, event | category | flops | bytes accessed | tf_op | source)
XLA Modules:
  0.0 192.9 jit_solution(5105689190015338644)
XLA Ops:
  0.6 3.1 %collective-permute-start.6 = (bf16[64,3072]{1,0:T(8,128)(2,1)}, bf16[64,3072]{1,0:T(8,128)(2,1)S(1)}, u32[]{:S(2)}, u32[]{:S(2)}) collective-permute-start(bf16[64,3072]{1,0:T(8,128)(2,1)} %refs_0_.1), channel_id=1, source_target_pairs={{0,2},{2,4},{4,6},{6,7},{7,5},{5,3},{3,1},{1,0},{8,10},{10,12},{12... | collective-permute-start | bytes 1179656 | tf_op jit(solution)/shard_map/ppermute | solution.py:497
  5.2 7.8 %collective-permute-done.6.refs_1_ = bf16[64,3072]{1,0:T(8,128)(2,1)S(1)} collective-permute-done((bf16[64,3072]{1,0:T(8,128)(2,1)}, bf16[64,3072]{1,0:T(8,128)(2,1)S(1)}, u32[]{:S(2)}, u32[]{:S(2)}) %collective-permute-start.6) | collective-permute-done | bytes 393248 | tf_op jit(solution)/shard_map/ppermute | solution.py:497
  13.0 1.8 collective-permute-start.7
  14.8 0.9 select_reduce_fusion
  16.6 1.3 collective-permute-start.1
  17.9 4.6 %collective-permute-start = (f32[200,128]{1,0:T(8,128)S(1)}, f32[200,128]{1,0:T(8,128)S(1)}, u32[]{:S(2)}, u32[]{:S(2)}) collective-permute-start(f32[200,128]{1,0:T(8,128)S(1)} %get-tuple-element.35), channel_id=1, source_target_pairs={{0,1},{1,2},{2,3},{3,4},{4,5},{5,6},{6,7},{8,9},{9,10},{10,11},{11... | collective-permute-start | bytes 307208 | tf_op jit(solution)/shard_map/ppermute | solution.py:29
  22.4 1.2 collective-permute-start.5
  24.8 1.8 collective-permute-done.1
  26.6 1.3 collective-permute-start.3
  28.8 3.0 %collective-permute-start.2 = (f32[3,200,128]{2,1,0:T(8,128)S(1)}, f32[3,200,128]{2,1,0:T(8,128)S(1)}, u32[]{:S(2)}, u32[]{:S(2)}) collective-permute-start(f32[3,200,128]{2,1,0:T(8,128)S(1)} %pad_maximum_fusion.mid_ref.refs_5_), channel_id=1, source_target_pairs={{0,8},{8,16},{16,24},{1,9},{9,17},{17,25},{2,10},{10,18},{18,26},{... | collective-permute-start | bytes 921608 | tf_op jit(solution)/shard_map/ppermute | solution.py:29
  32.4 2.6 %collective-permute-start.9 = (bf16[64,3072]{1,0:T(8,128)(2,1)}, bf16[64,3072]{1,0:T(8,128)(2,1)S(1)}, u32[]{:S(2)}, u32[]{:S(2)}) collective-permute-start(bf16[64,3072]{1,0:T(8,128)(2,1)} %collective-permute-done.5.refs_0_), channel_id=1, source_target_pairs={{2,0},{4,2},{6,4},{7,6},{5,7},{3,5},{1,3},{0,1},{10,8},{12,10},{14... | collective-permute-start | bytes 1179656 | tf_op jit(solution)/shard_map/ppermute | solution.py:501
  35.1 1.4 copy-done.3
  36.5 3.7 %copy-done.5 = bf16[3072,1536]{1,0:T(8,128)(2,1)S(1)} copy-done((bf16[3072,1536]{1,0:T(8,128)(2,1)S(1)}, bf16[3072,1536]{1,0:T(8,128)(2,1)}, u32[]{:S(2)}) %copy-start.5) | copy-done | bytes 9437208
  40.1 1.0 copy-done.9
  41.1 1.0 copy-done.11
  42.9 6.0 %context_field.2 = (f32[1,12,128]{2,1,0:T(8,128)S(1)}, bf16[3072,256]{1,0:T(8,128)(2,1)S(1)}) custom-call(s32[5]{0:T(128)S(1)} %stack.83.at_ref, bf16[64,3072]{1,0:T(8,128)(2,1)S(1)} %copy-done.9, bf16[64,3072]{1,0:T(8,128)(2,1)S(1)} %collective-permute-done.6.refs_1_, bf16[64,3072]{1,0:T(8,128)(2,1)S(1)} %collective-permute-done.4.refs_2_, ...), custom_call_target="tpu_custom_call" | custom-call | tf_op jit(solution)/shard_map/context_field/pallas_call | solution.py:409
  48.9 1.2 copy-done.6
  50.1 7.7 %context_field.3 = (f32[32,12,128]{2,1,0:T(8,128)}, bf16[3072,256]{1,0:T(8,128)(2,1)S(1)}) custom-call(s32[5]{0:T(128)S(1)} %stack.83.at_ref, bf16[64,3072]{1,0:T(8,128)(2,1)} %collective-permute-done.5.refs_0_, bf16[64,3072]{1,0:T(8,128)(2,1)} %collective-permute-done.8.refs_1_, bf16[64,3072]{1,0:T(8,128)(2,1)S(1)} %collective-permute-done.9.refs_2_, ...), custom_call_target="tpu_custom_call" | custom-call | tf_op jit(solution)/shard_map/context_field/pallas_call | solution.py:409
  57.8 1.2 copy-done.7
  59.0 8.6 %all-to-all-start = ((f32[32,12,128]{2,1,0:T(8,128)}), f32[32,12,128]{2,1,0:T(8,128)S(1)}, u32[]{:S(2)}, u32[]{:S(2)}) async-start(f32[32,12,128]{2,1,0:T(8,128)} %get-tuple-element.16), calls=%async_computation | async-start | bytes 524288 | tf_op jit(solution)/shard_map/all_to_all | solution.py:544
  67.6 8.6 %pair_weights.1 = (bf16[32,1536,128]{2,1,0:T(8,128)(2,1)S(1)}, f32[3,288,128]{2,1,0:T(8,128)S(1)}) custom-call(s32[5]{0:T(128)S(1)} %stack.83.at_ref, s32[32,12]{1,0:T(8,128)S(1)} %bitcast.68, f32[3,200,128]{2,1,0:T(8,128)S(1)} %collective-permute-done.2.low_ref.refs_4_, f32[3,200,128]{2,1,0:T(8,128)S(1)} %pad_maximum_fusion.mid_ref.refs_5_, ...), custom_call_target="tpu_custom_call" | custom-call | tf_op jit(solution)/shard_map/pair_weights/pallas_call | solution.py:154
  76.3 4.8 %copy-done = bf16[32,1536,128]{2,1,0:T(8,128)(2,1)} copy-done((bf16[32,1536,128]{2,1,0:T(8,128)(2,1)}, bf16[32,1536,128]{2,1,0:T(8,128)(2,1)S(1)}, u32[]{:S(2)}) %copy-start) | copy-done | bytes 12582936
  81.1 4.6 %copy-done.1 = bf16[32,1536,128]{2,1,0:T(8,128)(2,1)S(1)} copy-done((bf16[32,1536,128]{2,1,0:T(8,128)(2,1)S(1)}, bf16[32,1536,128]{2,1,0:T(8,128)(2,1)}, u32[]{:S(2)}) %copy-start.1) | copy-done | bytes 12582936
  85.7 8.0 %sweep.4 = (f32[96,128]{1,0:T(8,128)S(1)}, f32[96,128]{1,0:T(8,128)S(1)}, f32[12,128]{1,0:T(8,128)S(1)}) custom-call(s32[5]{0:T(128)S(1)} %stack.83.at_ref, s32[32,12]{1,0:T(8,128)S(1)} %bitcast.69, s32[2,9,16]{2,1,0:T(8,128)S(1)} %pad_add_fusion.refs_0_, f32[9,16]{1,0:T(8,128)S(1)} %bitcast.84, f32[32,12,128]{2,1,0:T(8,128)S(1)} %all-to-all-done.refs_2_, ...), custom_call_target="tpu_custom_call" | custom-call | tf_op jit(solution)/shard_map/sweep/pallas_call | solution.py:325
  93.7 1.3 collective-permute-start.12
  95.0 4.5 %collective-permute-start.11 = (f32[96,128]{1,0:T(8,128)S(1)}, f32[96,128]{1,0:T(8,128)S(1)}, u32[]{:S(2)}, u32[]{:S(2)}) collective-permute-start(f32[96,128]{1,0:T(8,128)S(1)} %get-tuple-element.18), channel_id=1, source_target_pairs={{0,1},{1,2},{2,3},{3,4},{4,5},{5,6},{6,7},{8,9},{9,10},{10,11},{11... | collective-permute-start | bytes 147464 | tf_op jit(solution)/shard_map/ppermute | solution.py:29
  99.6 1.6 collective-permute-done.11
  101.3 1.3 collective-permute-start.14
  102.6 3.0 %collective-permute-start.13 = (f32[3,96,128]{2,1,0:T(8,128)S(1)}, f32[3,96,128]{2,1,0:T(8,128)S(1)}, u32[]{:S(2)}, u32[]{:S(2)}) collective-permute-start(f32[3,96,128]{2,1,0:T(8,128)S(1)} %pad_maximum_fusion.1.refs_2_), channel_id=1, source_target_pairs={{0,8},{8,16},{16,24},{1,9},{9,17},{17,25},{2,10},{10,18},{18,26},{... | collective-permute-start | bytes 442376 | tf_op jit(solution)/shard_map/ppermute | solution.py:29
  105.6 1.0 collective-permute-done.13.refs_1_
  106.6 5.1 %sweep.5 = f32[96,128]{1,0:T(8,128)S(1)} custom-call(s32[5]{0:T(128)S(1)} %stack.83.at_ref, s32[32,12]{1,0:T(8,128)S(1)} %bitcast.70, f32[3,288,128]{2,1,0:T(8,128)S(1)} %get-tuple-element.14.refs_3_.refs_0_.refs_1_, f32[3,96,128]{2,1,0:T(8,128)S(1)} %collective-permute-done.13.refs_1_, f32[3,96,128]{2,1,0:T(8,128)S(1)} %pad_maximum_fusion.1.refs_2_, ...), custom_call_target="tpu_custom_call" | custom-call | tf_op jit(solution)/shard_map/sweep/pallas_call | solution.py:325
  111.7 1.3 collective-permute-start.16
  113.0 5.2 %collective-permute-start.15 = (f32[96,128]{1,0:T(8,128)S(1)}, f32[96,128]{1,0:T(8,128)S(1)}, u32[]{:S(2)}, u32[]{:S(2)}) collective-permute-start(f32[96,128]{1,0:T(8,128)S(1)} %sweep.5), channel_id=1, source_target_pairs={{0,1},{1,2},{2,3},{3,4},{4,5},{5,6},{6,7},{8,9},{9,10},{10,11},{11... | collective-permute-start | bytes 147464 | tf_op jit(solution)/shard_map/ppermute | solution.py:29
  118.4 1.6 collective-permute-done.15
  120.0 1.3 collective-permute-start.18
  121.3 3.9 %collective-permute-start.17 = (f32[3,96,128]{2,1,0:T(8,128)S(1)}, f32[3,96,128]{2,1,0:T(8,128)S(1)}, u32[]{:S(2)}, u32[]{:S(2)}) collective-permute-start(f32[3,96,128]{2,1,0:T(8,128)S(1)} %pad_maximum_fusion.2.refs_2_), channel_id=1, source_target_pairs={{0,8},{8,16},{16,24},{1,9},{9,17},{17,25},{2,10},{10,18},{18,26},{... | collective-permute-start | bytes 442376 | tf_op jit(solution)/shard_map/ppermute | solution.py:29
  125.2 1.0 collective-permute-done.17.refs_1_
  126.2 5.1 %sweep.6 = f32[96,128]{1,0:T(8,128)S(1)} custom-call(s32[5]{0:T(128)S(1)} %stack.83.at_ref, s32[32,12]{1,0:T(8,128)S(1)} %bitcast.71, f32[3,288,128]{2,1,0:T(8,128)S(1)} %get-tuple-element.14.refs_3_.refs_0_.refs_1_, f32[3,96,128]{2,1,0:T(8,128)S(1)} %collective-permute-done.17.refs_1_, f32[3,96,128]{2,1,0:T(8,128)S(1)} %pad_maximum_fusion.2.refs_2_, ...), custom_call_target="tpu_custom_call" | custom-call | tf_op jit(solution)/shard_map/sweep/pallas_call | solution.py:325
  131.3 1.3 collective-permute-start.20
  132.6 5.8 %collective-permute-start.19 = (f32[96,128]{1,0:T(8,128)S(1)}, f32[96,128]{1,0:T(8,128)S(1)}, u32[]{:S(2)}, u32[]{:S(2)}) collective-permute-start(f32[96,128]{1,0:T(8,128)S(1)} %sweep.6), channel_id=1, source_target_pairs={{0,1},{1,2},{2,3},{3,4},{4,5},{5,6},{6,7},{8,9},{9,10},{10,11},{11... | collective-permute-start | bytes 147464 | tf_op jit(solution)/shard_map/ppermute | solution.py:29
  138.5 1.6 collective-permute-done.19
  140.1 1.3 collective-permute-start.22
  141.4 6.1 %collective-permute-start.21 = (f32[3,96,128]{2,1,0:T(8,128)S(1)}, f32[3,96,128]{2,1,0:T(8,128)S(1)}, u32[]{:S(2)}, u32[]{:S(2)}) collective-permute-start(f32[3,96,128]{2,1,0:T(8,128)S(1)} %pad_maximum_fusion.3.refs_3_), channel_id=1, source_target_pairs={{0,8},{8,16},{16,24},{1,9},{9,17},{17,25},{2,10},{10,18},{18,26},{... | collective-permute-start | bytes 442376 | tf_op jit(solution)/shard_map/ppermute | solution.py:29
  147.5 1.0 collective-permute-done.21.refs_2_
  148.5 6.1 %sweep.7 = (f32[96,128]{1,0:T(8,128)}, f32[32,16,128]{2,1,0:T(8,128)}) custom-call(s32[5]{0:T(128)S(1)} %stack.83.at_ref, s32[32,12]{1,0:T(8,128)S(1)} %bitcast.72, s32[16]{0:T(128)S(1)} %bitcast.86, f32[3,288,128]{2,1,0:T(8,128)S(1)} %get-tuple-element.14.refs_3_.refs_0_.refs_1_, f32[3,96,128]{2,1,0:T(8,128)S(1)} %collective-permute-done.21.refs_2_, ...), custom_call_target="tpu_custom_call" | custom-call | tf_op jit(solution)/shard_map/sweep/pallas_call | solution.py:325
  154.6 14.5 %all-to-all-start.1 = ((f32[32,16,128]{2,1,0:T(8,128)}), f32[32,16,128]{2,1,0:T(8,128)S(1)}, u32[]{:S(2)}, u32[]{:S(2)}) async-start(f32[32,16,128]{2,1,0:T(8,128)} %get-tuple-element.24), calls=%async_computation.1 | async-start | bytes 524288 | tf_op jit(solution)/shard_map/all_to_all | solution.py:559
  169.7 9.8 %all-to-all-done.1 = f32[32,16,128]{2,1,0:T(8,128)S(1)} async-done(((f32[32,16,128]{2,1,0:T(8,128)}), f32[32,16,128]{2,1,0:T(8,128)S(1)}, u32[]{:S(2)}, u32[]{:S(2)}) %all-to-all-start.1) | async-done | bytes 262176 | tf_op jit(solution)/shard_map/all_to_all | solution.py:559
  180.2 12.7 %fock_term.1 = f32[3072,1536]{1,0:T(8,128)} custom-call(s32[5]{0:T(128)} %copy-done.14, bf16[3072,256]{1,0:T(8,128)(2,1)} %copy-done.6, bf16[3072,256]{1,0:T(8,128)(2,1)} %copy-done.7, bf16[512,1536]{1,0:T(8,128)(2,1)} %refs_2_.1, f32[3,1536]{1,0:T(4,128)} %refs_3_.1, f32[512,128]{1,0:T(8,128)} %bitcast.87), custom_call_target="tpu_custom_call" | custom-call | tf_op jit(solution)/shard_map/fock_term/pallas_call | solution.py:460
  (65 shorter events, 7.6 us)
Async XLA Ops:
  0.6 12.4 %collective-permute-start.6 = (bf16[64,3072]{1,0:T(8,128)(2,1)}, bf16[64,3072]{1,0:T(8,128)(2,1)S(1)}, u32[]{:S(2)}, u32[]{:S(2)}) collective-permute-start(bf16[64,3072]{1,0:T(8,128)(2,1)} %refs_0_.1), channel_id=1, source_target_pairs={{0,2},{2,4},{4,6},{6,7},{7,5},{5,3},{3,1},{1,0},{8,10},{10,12},{12... | collective-permute-start | bytes 1179656 | tf_op jit(solution)/shard_map/ppermute | solution.py:497
  3.7 18.7 %collective-permute-start.4 = (bf16[64,3072]{1,0:T(8,128)(2,1)}, bf16[64,3072]{1,0:T(8,128)(2,1)S(1)}, u32[]{:S(2)}, u32[]{:S(2)}) collective-permute-start(bf16[64,3072]{1,0:T(8,128)(2,1)} %refs_0_.1), channel_id=1, source_target_pairs={{2,0},{4,2},{6,4},{7,6},{5,7},{3,5},{1,3},{0,1},{10,8},{12,10},{14... | collective-permute-start | bytes 1179656 | tf_op jit(solution)/shard_map/ppermute | solution.py:501
  13.0 11.4 %collective-permute-start.7 = (bf16[64,3072]{1,0:T(8,128)(2,1)S(1)}, bf16[64,3072]{1,0:T(8,128)(2,1)S(1)}, u32[]{:S(2)}, u32[]{:S(2)}) collective-permute-start(bf16[64,3072]{1,0:T(8,128)(2,1)S(1)} %collective-permute-done.6.refs_1_), channel_id=1, source_target_pairs={{0,2},{2,4},{4,6},{6,7},{7,5},{5,3},{3,1},{1,0},{8,10},{10,12},{12... | collective-permute-start | bytes 1179656 | tf_op jit(solution)/shard_map/ppermute | solution.py:497
  16.6 10.0 %collective-permute-start.1 = (f32[200,128]{1,0:T(8,128)S(1)}, f32[200,128]{1,0:T(8,128)S(1)}, u32[]{:S(2)}, u32[]{:S(2)}) collective-permute-start(f32[200,128]{1,0:T(8,128)S(1)} %get-tuple-element.35), channel_id=1, source_target_pairs={{1,0},{2,1},{3,2},{4,3},{5,4},{6,5},{7,6},{9,8},{10,9},{11,10},{12... | collective-permute-start | bytes 307208 | tf_op jit(solution)/shard_map/ppermute | solution.py:29
  17.9 8.7 %collective-permute-start = (f32[200,128]{1,0:T(8,128)S(1)}, f32[200,128]{1,0:T(8,128)S(1)}, u32[]{:S(2)}, u32[]{:S(2)}) collective-permute-start(f32[200,128]{1,0:T(8,128)S(1)} %get-tuple-element.35), channel_id=1, source_target_pairs={{0,1},{1,2},{2,3},{3,4},{4,5},{5,6},{6,7},{8,9},{9,10},{10,11},{11... | collective-permute-start | bytes 307208 | tf_op jit(solution)/shard_map/ppermute | solution.py:29
  22.4 10.0 %collective-permute-start.5 = (bf16[64,3072]{1,0:T(8,128)(2,1)S(1)}, bf16[64,3072]{1,0:T(8,128)(2,1)}, u32[]{:S(2)}, u32[]{:S(2)}) collective-permute-start(bf16[64,3072]{1,0:T(8,128)(2,1)S(1)} %collective-permute-done.4.refs_2_), channel_id=1, source_target_pairs={{2,0},{4,2},{6,4},{7,6},{5,7},{3,5},{1,3},{0,1},{10,8},{12,10},{14... | collective-permute-start | bytes 1179656 | tf_op jit(solution)/shard_map/ppermute | solution.py:501
  24.4 10.6 %copy-start.10 = (bf16[64,3072]{1,0:T(8,128)(2,1)}, bf16[64,3072]{1,0:T(8,128)(2,1)S(1)}, u32[]{:S(2)}) copy-start(bf16[64,3072]{1,0:T(8,128)(2,1)S(1)} %collective-permute-done.7.refs_3_) | copy-start | bytes 1179652
  24.4 10.6 %collective-permute-start.8 = (bf16[64,3072]{1,0:T(8,128)(2,1)S(1)}, bf16[64,3072]{1,0:T(8,128)(2,1)}, u32[]{:S(2)}, u32[]{:S(2)}) collective-permute-start(bf16[64,3072]{1,0:T(8,128)(2,1)S(1)} %collective-permute-done.7.refs_3_), channel_id=1, source_target_pairs={{0,2},{2,4},{4,6},{6,7},{7,5},{5,3},{3,1},{1,0},{8,10},{10,12},{12... | collective-permute-start | bytes 1179656 | tf_op jit(solution)/shard_map/ppermute | solution.py:497
  26.6 8.4 %collective-permute-start.3 = (f32[3,200,128]{2,1,0:T(8,128)S(1)}, f32[3,200,128]{2,1,0:T(8,128)S(1)}, u32[]{:S(2)}, u32[]{:S(2)}) collective-permute-start(f32[3,200,128]{2,1,0:T(8,128)S(1)} %pad_maximum_fusion.mid_ref.refs_5_), channel_id=1, source_target_pairs={{8,0},{16,8},{24,16},{9,1},{17,9},{25,17},{10,2},{18,10},{26,18},{... | collective-permute-start | bytes 921608 | tf_op jit(solution)/shard_map/ppermute | solution.py:29
  28.8 119.7 %copy-start.14 = (s32[5]{0:T(128)}, s32[5]{0:T(128)S(1)}, u32[]{:S(2)}) copy-start(s32[5]{0:T(128)S(1)} %stack.83.at_ref) | copy-start | bytes 64
  28.8 6.2 %collective-permute-start.2 = (f32[3,200,128]{2,1,0:T(8,128)S(1)}, f32[3,200,128]{2,1,0:T(8,128)S(1)}, u32[]{:S(2)}, u32[]{:S(2)}) collective-permute-start(f32[3,200,128]{2,1,0:T(8,128)S(1)} %pad_maximum_fusion.mid_ref.refs_5_), channel_id=1, source_target_pairs={{0,8},{8,16},{16,24},{1,9},{9,17},{17,25},{2,10},{10,18},{18,26},{... | collective-permute-start | bytes 921608 | tf_op jit(solution)/shard_map/ppermute | solution.py:29
  32.4 17.7 %collective-permute-start.9 = (bf16[64,3072]{1,0:T(8,128)(2,1)}, bf16[64,3072]{1,0:T(8,128)(2,1)S(1)}, u32[]{:S(2)}, u32[]{:S(2)}) collective-permute-start(bf16[64,3072]{1,0:T(8,128)(2,1)} %collective-permute-done.5.refs_0_), channel_id=1, source_target_pairs={{2,0},{4,2},{6,4},{7,6},{5,7},{3,5},{1,3},{0,1},{10,8},{12,10},{14... | collective-permute-start | bytes 1179656 | tf_op jit(solution)/shard_map/ppermute | solution.py:501
  35.0 15.1 %collective-permute-start.10 = (bf16[64,3072]{1,0:T(8,128)(2,1)}, bf16[64,3072]{1,0:T(8,128)(2,1)S(1)}, u32[]{:S(2)}, u32[]{:S(2)}) collective-permute-start(bf16[64,3072]{1,0:T(8,128)(2,1)} %collective-permute-done.8.refs_1_), channel_id=1, source_target_pairs={{0,2},{2,4},{4,6},{6,7},{7,5},{5,3},{3,1},{1,0},{8,10},{10,12},{12... | collective-permute-start | bytes 1179656 | tf_op jit(solution)/shard_map/ppermute | solution.py:497
  35.0 1.4 copy-start.3
  36.5 3.7 %copy-start.5 = (bf16[3072,1536]{1,0:T(8,128)(2,1)S(1)}, bf16[3072,1536]{1,0:T(8,128)(2,1)}, u32[]{:S(2)}) copy-start(bf16[3072,1536]{1,0:T(8,128)(2,1)} %refs_4_.3) | copy-start | bytes 28311556
  40.1 1.0 copy-start.9
  41.1 1.0 copy-start.11
  42.1 0.7 copy-start.12
  42.9 7.2 %copy-start.4 = (bf16[512,1536]{1,0:T(8,128)(2,1)S(1)}, bf16[512,1536]{1,0:T(8,128)(2,1)}, u32[]{:S(2)}) copy-start(bf16[512,1536]{1,0:T(8,128)(2,1)} %refs_2_.1) | copy-start | bytes 4718596
  48.9 1.2 copy-start.6
  50.1 31.0 %copy-start.8 = (f32[1,1,4096]{2,1,0:T(1,128)S(1)}, f32[1,1,4096]{2,1,0:T(1,128)}, u32[]{:S(2)}) copy-start(f32[1,1,4096]{2,1,0:T(1,128)} %param.14) | copy-start | bytes 49156
  50.1 31.0 %copy-start.13 = (f32[3,1,1,4096]{3,2,1,0:T(1,128)S(1)}, f32[3,1,1,4096]{3,2,1,0:T(1,128)}, u32[]{:S(2)}) copy-start(f32[3,1,1,4096]{3,2,1,0:T(1,128)} %param.15) | copy-start | bytes 147460
  57.8 1.2 copy-start.7
  59.0 22.1 %all-to-all-start = ((f32[32,12,128]{2,1,0:T(8,128)}), f32[32,12,128]{2,1,0:T(8,128)S(1)}, u32[]{:S(2)}, u32[]{:S(2)}) async-start(f32[32,12,128]{2,1,0:T(8,128)} %get-tuple-element.16), calls=%async_computation | async-start | bytes 524288 | tf_op jit(solution)/shard_map/all_to_all | solution.py:544
  76.3 4.8 %copy-start = (bf16[32,1536,128]{2,1,0:T(8,128)(2,1)}, bf16[32,1536,128]{2,1,0:T(8,128)(2,1)S(1)}, u32[]{:S(2)}) copy-start(bf16[32,1536,128]{2,1,0:T(8,128)(2,1)S(1)} %get-tuple-element.17.refs_7_.refs_4_.refs_5_) | copy-start | bytes 37748740
  81.1 4.6 %copy-start.1 = (bf16[32,1536,128]{2,1,0:T(8,128)(2,1)S(1)}, bf16[32,1536,128]{2,1,0:T(8,128)(2,1)}, u32[]{:S(2)}) copy-start(bf16[32,1536,128]{2,1,0:T(8,128)(2,1)} %copy-done) | copy-start | bytes 37748740
  85.7 20.9 %copy-start.2 = (bf16[32,1536,128]{2,1,0:T(8,128)(2,1)S(1)}, bf16[32,1536,128]{2,1,0:T(8,128)(2,1)}, u32[]{:S(2)}) copy-start(bf16[32,1536,128]{2,1,0:T(8,128)(2,1)} %copy-done) | copy-start | bytes 37748740
  93.7 6.0 %collective-permute-start.12 = (f32[96,128]{1,0:T(8,128)S(1)}, f32[96,128]{1,0:T(8,128)S(1)}, u32[]{:S(2)}, u32[]{:S(2)}) collective-permute-start(f32[96,128]{1,0:T(8,128)S(1)} %get-tuple-element.18), channel_id=1, source_target_pairs={{1,0},{2,1},{3,2},{4,3},{5,4},{6,5},{7,6},{9,8},{10,9},{11,10},{12... | collective-permute-start | bytes 147464 | tf_op jit(solution)/shard_map/ppermute | solution.py:29
  95.0 6.3 %collective-permute-start.11 = (f32[96,128]{1,0:T(8,128)S(1)}, f32[96,128]{1,0:T(8,128)S(1)}, u32[]{:S(2)}, u32[]{:S(2)}) collective-permute-start(f32[96,128]{1,0:T(8,128)S(1)} %get-tuple-element.18), channel_id=1, source_target_pairs={{0,1},{1,2},{2,3},{3,4},{4,5},{5,6},{6,7},{8,9},{9,10},{10,11},{11... | collective-permute-start | bytes 147464 | tf_op jit(solution)/shard_map/ppermute | solution.py:29
  101.3 4.3 %collective-permute-start.14 = (f32[3,96,128]{2,1,0:T(8,128)S(1)}, f32[3,96,128]{2,1,0:T(8,128)S(1)}, u32[]{:S(2)}, u32[]{:S(2)}) collective-permute-start(f32[3,96,128]{2,1,0:T(8,128)S(1)} %pad_maximum_fusion.1.refs_2_), channel_id=1, source_target_pairs={{8,0},{16,8},{24,16},{9,1},{17,9},{25,17},{10,2},{18,10},{26,18},{... | collective-permute-start | bytes 442376 | tf_op jit(solution)/shard_map/ppermute | solution.py:29
  102.6 4.0 %collective-permute-start.13 = (f32[3,96,128]{2,1,0:T(8,128)S(1)}, f32[3,96,128]{2,1,0:T(8,128)S(1)}, u32[]{:S(2)}, u32[]{:S(2)}) collective-permute-start(f32[3,96,128]{2,1,0:T(8,128)S(1)} %pad_maximum_fusion.1.refs_2_), channel_id=1, source_target_pairs={{0,8},{8,16},{16,24},{1,9},{9,17},{17,25},{2,10},{10,18},{18,26},{... | collective-permute-start | bytes 442376 | tf_op jit(solution)/shard_map/ppermute | solution.py:29
  111.7 36.8 %copy-start.15 = (s32[1,1,16]{2,1,0:T(1,128)S(1)}, s32[1,1,16]{2,1,0:T(1,128)}, u32[]{:S(2)}) copy-start(s32[1,1,16]{2,1,0:T(1,128)} %param.17) | copy-start | bytes 196
  111.7 6.6 %collective-permute-start.16 = (f32[96,128]{1,0:T(8,128)S(1)}, f32[96,128]{1,0:T(8,128)S(1)}, u32[]{:S(2)}, u32[]{:S(2)}) collective-permute-start(f32[96,128]{1,0:T(8,128)S(1)} %sweep.5), channel_id=1, source_target_pairs={{1,0},{2,1},{3,2},{4,3},{5,4},{6,5},{7,6},{9,8},{10,9},{11,10},{12... | collective-permute-start | bytes 147464 | tf_op jit(solution)/shard_map/ppermute | solution.py:29
  113.0 6.9 %collective-permute-start.15 = (f32[96,128]{1,0:T(8,128)S(1)}, f32[96,128]{1,0:T(8,128)S(1)}, u32[]{:S(2)}, u32[]{:S(2)}) collective-permute-start(f32[96,128]{1,0:T(8,128)S(1)} %sweep.5), channel_id=1, source_target_pairs={{0,1},{1,2},{2,3},{3,4},{4,5},{5,6},{6,7},{8,9},{9,10},{10,11},{11... | collective-permute-start | bytes 147464 | tf_op jit(solution)/shard_map/ppermute | solution.py:29
  120.0 5.2 %collective-permute-start.18 = (f32[3,96,128]{2,1,0:T(8,128)S(1)}, f32[3,96,128]{2,1,0:T(8,128)S(1)}, u32[]{:S(2)}, u32[]{:S(2)}) collective-permute-start(f32[3,96,128]{2,1,0:T(8,128)S(1)} %pad_maximum_fusion.2.refs_2_), channel_id=1, source_target_pairs={{8,0},{16,8},{24,16},{9,1},{17,9},{25,17},{10,2},{18,10},{26,18},{... | collective-permute-start | bytes 442376 | tf_op jit(solution)/shard_map/ppermute | solution.py:29
  121.3 4.9 %collective-permute-start.17 = (f32[3,96,128]{2,1,0:T(8,128)S(1)}, f32[3,96,128]{2,1,0:T(8,128)S(1)}, u32[]{:S(2)}, u32[]{:S(2)}) collective-permute-start(f32[3,96,128]{2,1,0:T(8,128)S(1)} %pad_maximum_fusion.2.refs_2_), channel_id=1, source_target_pairs={{0,8},{8,16},{16,24},{1,9},{9,17},{17,25},{2,10},{10,18},{18,26},{... | collective-permute-start | bytes 442376 | tf_op jit(solution)/shard_map/ppermute | solution.py:29
  131.3 7.2 %collective-permute-start.20 = (f32[96,128]{1,0:T(8,128)S(1)}, f32[96,128]{1,0:T(8,128)S(1)}, u32[]{:S(2)}, u32[]{:S(2)}) collective-permute-start(f32[96,128]{1,0:T(8,128)S(1)} %sweep.6), channel_id=1, source_target_pairs={{1,0},{2,1},{3,2},{4,3},{5,4},{6,5},{7,6},{9,8},{10,9},{11,10},{12... | collective-permute-start | bytes 147464 | tf_op jit(solution)/shard_map/ppermute | solution.py:29
  132.6 7.5 %collective-permute-start.19 = (f32[96,128]{1,0:T(8,128)S(1)}, f32[96,128]{1,0:T(8,128)S(1)}, u32[]{:S(2)}, u32[]{:S(2)}) collective-permute-start(f32[96,128]{1,0:T(8,128)S(1)} %sweep.6), channel_id=1, source_target_pairs={{0,1},{1,2},{2,3},{3,4},{4,5},{5,6},{6,7},{8,9},{9,10},{10,11},{11... | collective-permute-start | bytes 147464 | tf_op jit(solution)/shard_map/ppermute | solution.py:29
  140.1 7.4 %collective-permute-start.22 = (f32[3,96,128]{2,1,0:T(8,128)S(1)}, f32[3,96,128]{2,1,0:T(8,128)S(1)}, u32[]{:S(2)}, u32[]{:S(2)}) collective-permute-start(f32[3,96,128]{2,1,0:T(8,128)S(1)} %pad_maximum_fusion.3.refs_3_), channel_id=1, source_target_pairs={{8,0},{16,8},{24,16},{9,1},{17,9},{25,17},{10,2},{18,10},{26,18},{... | collective-permute-start | bytes 442376 | tf_op jit(solution)/shard_map/ppermute | solution.py:29
  141.4 7.1 %collective-permute-start.21 = (f32[3,96,128]{2,1,0:T(8,128)S(1)}, f32[3,96,128]{2,1,0:T(8,128)S(1)}, u32[]{:S(2)}, u32[]{:S(2)}) collective-permute-start(f32[3,96,128]{2,1,0:T(8,128)S(1)} %pad_maximum_fusion.3.refs_3_), channel_id=1, source_target_pairs={{0,8},{8,16},{16,24},{1,9},{9,17},{17,25},{2,10},{10,18},{18,26},{... | collective-permute-start | bytes 442376 | tf_op jit(solution)/shard_map/ppermute | solution.py:29
  154.6 24.9 %all-to-all-start.1 = ((f32[32,16,128]{2,1,0:T(8,128)}), f32[32,16,128]{2,1,0:T(8,128)S(1)}, u32[]{:S(2)}, u32[]{:S(2)}) async-start(f32[32,16,128]{2,1,0:T(8,128)} %get-tuple-element.24), calls=%async_computation.1 | async-start | bytes 524288 | tf_op jit(solution)/shard_map/all_to_all | solution.py:559
  179.5 0.7 copy-start.16

commit v3 on v2

--- a/solution.py
+++ b/solution.py
@@ -170,10 +170,14 @@
     refs = list(refs)
     if first:
         spot_ref, polar_ref, parts_ref = refs.pop(0), refs.pop(0), refs.pop(0)
+    else:
+        own_ref = refs.pop(0)
     if last:
         target_ref = refs.pop(0)
     coords_ref, low_ref, mid_ref, high_ref, weights_ref, alpha_ref, total_ref, out_ref = refs[:8]
     refs = refs[8:]
+    if not last:
+        halo_ref = refs.pop(0)
     if first:
         sum_ref, field_ref = refs.pop(0), refs.pop(0)
     if last:
@@ -196,9 +200,9 @@
     for a, ref in enumerate((low_ref, mid_ref, high_ref)):
         for b in range(3):
             for k in range(3):
-                v_ref[k, (3 * a + b) * blocks : (3 * a + b + 1) * blocks, :] = ref[
-                    b, base + k * blocks : base + (k + 1) * blocks, :
-                ]
+                rows = slice(base + k * blocks, base + (k + 1) * blocks)
+                given = own_ref[rows, :] if (a, b) == (1, 1) and not first else ref[b, rows, :]
+                v_ref[k, (3 * a + b) * blocks : (3 * a + b + 1) * blocks, :] = given.astype(F32)
     if first:
         sum_ref[...] = total_ref[...]
         copy.wait()
@@ -284,7 +288,10 @@
         force = x[k] * inside - one + q[k] - (size * p[k] - 2.0 * other) * (1.0 / 3.0)
         rows = slice(k * blocks, (k + 1) * blocks)
         given = sum_ref[rows, :] if first else total_ref[rows, :]
-        out_ref[rows, :] = alpha * (given + (3.0 * COUPLING) * force)
+        value = alpha * (given + (3.0 * COUPLING) * force)
+        out_ref[rows, :] = value
+        if not last:
+            halo_ref[rows, :] = value.astype(BF16)
     if last:
         per_brick = target_ref.shape[0]
         for j in range(per_brick):
@@ -300,13 +307,13 @@
             pick_ref[i] = pick_ref[0]
 
 
-def sweep(at, links, coords, around, weights, alpha, total, tail=None, parts=None, target=None, copies=1):
+def sweep(at, links, coords, around, weights, alpha, total, tail=None, parts=None, own=None, target=None, copies=1):
     blocks, depth, width = weights.shape
     region = coords.shape[1]
     first, last = parts is not None, target is not None
     per_step = 8
     rows = jax.ShapeDtypeStruct((3 * blocks, width), F32)
-    outs = [rows]
+    outs = [rows] if last else [rows, jax.ShapeDtypeStruct((3 * blocks, width), BF16)]
     scratch = [
         pltpu.VMEM((3, region, width), F32),
         pltpu.VMEM((per_step, PARTS * TERMS, depth), BF16),
@@ -318,6 +325,9 @@
         given += [*tail, parts]
         specs += [SMEM, SMEM, VMEM]
         scratch += [pltpu.SMEM(parts.shape[1:], F32), pltpu.SemaphoreType.DMA]
+    else:
+        given.append(own)
+        specs.append(VMEM)
     if last:
         outs.append(jax.ShapeDtypeStruct((copies, target.shape[0], width), F32))
         given.append(target)
@@ -545,16 +555,25 @@
 
     alpha_rows = polar.reshape(blocks, width)
     total = fixed.reshape(3 * blocks, width)
-    current, total, field = sweep(
+    current, halo, total, field = sweep(
         at, links, coords, around, weights, alpha_rows, total, tail=(spots, tails[:, 1]), parts=parts
     )
     for repeat in range(1, SWEEPS):
-        around = exchange(current)
+        around = exchange(halo)
         if repeat < SWEEPS - 1:
-            current = sweep(at, links, coords, around, weights, alpha_rows, total)[0]
+            current, halo = sweep(at, links, coords, around, weights, alpha_rows, total, own=current)
         else:
             current, picks = sweep(
-                at, links, coords, around, weights, alpha_rows, total, target=own_targets, copies=devices
+                at,
+                links,
+                coords,
+                around,
+                weights,
+                alpha_rows,
+                total,
+                own=current,
+                target=own_targets,
+                copies=devices,
             )
     dipoles = lax.all_to_all(picks, BOTH, 0, 0).reshape(devices * per_brick, width)
     fock_polar = fock_term(at, parts_of, members, lefts, right_factor, directions, dipoles)

time: 194 us -> 191 us (0.985)
  starting transfers between devices: 78.6 us -> 76.4 us
  transfers between devices with their start and end apart: 25 -> 25, of which waited for: 14 -> 11; matrix products, arithmetic and copies ran while one was open for 2% -> 3% of each run, Pallas kernels for 8% -> 8%
where the time goes in v3:
time: 191 us; the launch traced here: 190 us
  starting transfers between devices  76.4 us (40%)
  Pallas kernels  59.3 us (31%)
  waiting for transfers between devices  27.8 us (15%)
  local copies, waits for them, and re-layouts  21.7 us (11%)
  other arithmetic  3.31 us (2%)
    ppermute x16, starting transfers between devices, shift(): return lax.ppermute(block, axis, pairs)  45.1 us
    pallas_call x4, Pallas kernels, sweep(): pl.pallas_call(functools.partial(sweep_kernel, per_step, blocks, first, l...  24.3 us
    unnamed x36, local copies, waits for them, and re-layouts  21 us
    pallas_call x2, Pallas kernels, context_field(): pl.pallas_call(functools.partial(context_kernel, count, offsets, members,...  13.7 us
    all_to_all x1, starting transfers between devices, on_device(): lax.all_to_all(picks, BOTH, 0, 0).reshape(devices * per_brick, width)  13.6 us
    pallas_call x1, Pallas kernels, fock_term(): pl.pallas_call(functools.partial(fock_kernel, groups, members), out_shape...  12.7 us
    all_to_all x1, waiting for transfers between devices, on_device(): lax.all_to_all(picks, BOTH, 0, 0).reshape(devices * per_brick, width)  9.76 us
    ppermute x16, waiting for transfers between devices, shift(): return lax.ppermute(block, axis, pairs)  8.93 us
  transfers between devices with their start and end apart: 25, of which 11 were waited for; matrix products, arithmetic and copies ran while one was open for 3% of the time, Pallas kernels for 8%

profile of v3, /device:TPU:0, one launch (start us, length us, event | category | flops | bytes accessed | tf_op | source)
XLA Modules:
  0.0 189.7 jit_solution(6153444181322578321)
XLA Ops:
  0.6 3.1 %collective-permute-start.6 = (bf16[64,3072]{1,0:T(8,128)(2,1)}, bf16[64,3072]{1,0:T(8,128)(2,1)S(1)}, u32[]{:S(2)}, u32[]{:S(2)}) collective-permute-start(bf16[64,3072]{1,0:T(8,128)(2,1)} %refs_0_.1), channel_id=1, source_target_pairs={{0,2},{2,4},{4,6},{6,7},{7,5},{5,3},{3,1},{1,0},{8,10},{10,12},{12... | collective-permute-start | bytes 1179656 | tf_op jit(solution)/shard_map/ppermute | solution.py:507
  5.2 7.8 %collective-permute-done.6.refs_1_ = bf16[64,3072]{1,0:T(8,128)(2,1)S(1)} collective-permute-done((bf16[64,3072]{1,0:T(8,128)(2,1)}, bf16[64,3072]{1,0:T(8,128)(2,1)S(1)}, u32[]{:S(2)}, u32[]{:S(2)}) %collective-permute-start.6) | collective-permute-done | bytes 393248 | tf_op jit(solution)/shard_map/ppermute | solution.py:507
  13.0 1.8 collective-permute-start.7
  14.8 0.9 select_reduce_fusion
  16.6 1.3 collective-permute-start.1
  17.9 4.6 %collective-permute-start = (f32[200,128]{1,0:T(8,128)S(1)}, f32[200,128]{1,0:T(8,128)S(1)}, u32[]{:S(2)}, u32[]{:S(2)}) collective-permute-start(f32[200,128]{1,0:T(8,128)S(1)} %get-tuple-element.45), channel_id=1, source_target_pairs={{0,1},{1,2},{2,3},{3,4},{4,5},{5,6},{6,7},{8,9},{9,10},{10,11},{11... | collective-permute-start | bytes 307208 | tf_op jit(solution)/shard_map/ppermute | solution.py:29
  22.4 1.2 collective-permute-start.5
  24.8 1.8 collective-permute-done.1
  26.6 1.3 collective-permute-start.3
  28.8 3.0 %collective-permute-start.2 = (f32[3,200,128]{2,1,0:T(8,128)S(1)}, f32[3,200,128]{2,1,0:T(8,128)S(1)}, u32[]{:S(2)}, u32[]{:S(2)}) collective-permute-start(f32[3,200,128]{2,1,0:T(8,128)S(1)} %pad_maximum_fusion.mid_ref.refs_5_), channel_id=1, source_target_pairs={{0,8},{8,16},{16,24},{1,9},{9,17},{17,25},{2,10},{10,18},{18,26},{... | collective-permute-start | bytes 921608 | tf_op jit(solution)/shard_map/ppermute | solution.py:29
  32.4 2.6 %collective-permute-start.9 = (bf16[64,3072]{1,0:T(8,128)(2,1)}, bf16[64,3072]{1,0:T(8,128)(2,1)S(1)}, u32[]{:S(2)}, u32[]{:S(2)}) collective-permute-start(bf16[64,3072]{1,0:T(8,128)(2,1)} %collective-permute-done.5.refs_0_), channel_id=1, source_target_pairs={{2,0},{4,2},{6,4},{7,6},{5,7},{3,5},{1,3},{0,1},{10,8},{12,10},{14... | collective-permute-start | bytes 1179656 | tf_op jit(solution)/shard_map/ppermute | solution.py:511
  35.1 1.4 copy-done.3
  36.5 3.7 %copy-done.5 = bf16[3072,1536]{1,0:T(8,128)(2,1)S(1)} copy-done((bf16[3072,1536]{1,0:T(8,128)(2,1)S(1)}, bf16[3072,1536]{1,0:T(8,128)(2,1)}, u32[]{:S(2)}) %copy-start.5) | copy-done | bytes 9437208
  40.1 1.0 copy-done.9
  41.1 1.0 copy-done.11
  42.9 6.0 %context_field.2 = (f32[1,12,128]{2,1,0:T(8,128)S(1)}, bf16[3072,256]{1,0:T(8,128)(2,1)S(1)}) custom-call(s32[5]{0:T(128)S(1)} %stack.83.at_ref, bf16[64,3072]{1,0:T(8,128)(2,1)S(1)} %copy-done.9, bf16[64,3072]{1,0:T(8,128)(2,1)S(1)} %collective-permute-done.6.refs_1_, bf16[64,3072]{1,0:T(8,128)(2,1)S(1)} %collective-permute-done.4.refs_2_, ...), custom_call_target="tpu_custom_call" | custom-call | tf_op jit(solution)/shard_map/context_field/pallas_call | solution.py:419
  48.9 1.2 copy-done.6
  50.1 7.7 %context_field.3 = (f32[32,12,128]{2,1,0:T(8,128)}, bf16[3072,256]{1,0:T(8,128)(2,1)S(1)}) custom-call(s32[5]{0:T(128)S(1)} %stack.83.at_ref, bf16[64,3072]{1,0:T(8,128)(2,1)} %collective-permute-done.5.refs_0_, bf16[64,3072]{1,0:T(8,128)(2,1)} %collective-permute-done.8.refs_1_, bf16[64,3072]{1,0:T(8,128)(2,1)S(1)} %collective-permute-done.9.refs_2_, ...), custom_call_target="tpu_custom_call" | custom-call | tf_op jit(solution)/shard_map/context_field/pallas_call | solution.py:419
  57.8 1.1 copy-done.7
  59.0 8.6 %all-to-all-start = ((f32[32,12,128]{2,1,0:T(8,128)}), f32[32,12,128]{2,1,0:T(8,128)S(1)}, u32[]{:S(2)}, u32[]{:S(2)}) async-start(f32[32,12,128]{2,1,0:T(8,128)} %get-tuple-element.20), calls=%async_computation | async-start | bytes 524288 | tf_op jit(solution)/shard_map/all_to_all | solution.py:554
  67.6 8.6 %pair_weights.1 = (bf16[32,1536,128]{2,1,0:T(8,128)(2,1)S(1)}, f32[3,288,128]{2,1,0:T(8,128)S(1)}) custom-call(s32[5]{0:T(128)S(1)} %stack.83.at_ref, s32[32,12]{1,0:T(8,128)S(1)} %bitcast.68, f32[3,200,128]{2,1,0:T(8,128)S(1)} %collective-permute-done.2.low_ref.refs_4_, f32[3,200,128]{2,1,0:T(8,128)S(1)} %pad_maximum_fusion.mid_ref.refs_5_, ...), custom_call_target="tpu_custom_call" | custom-call | tf_op jit(solution)/shard_map/pair_weights/pallas_call | solution.py:154
  76.3 4.8 %copy-done = bf16[32,1536,128]{2,1,0:T(8,128)(2,1)} copy-done((bf16[32,1536,128]{2,1,0:T(8,128)(2,1)}, bf16[32,1536,128]{2,1,0:T(8,128)(2,1)S(1)}, u32[]{:S(2)}) %copy-start) | copy-done | bytes 12582936
  81.1 4.6 %copy-done.1 = bf16[32,1536,128]{2,1,0:T(8,128)(2,1)S(1)} copy-done((bf16[32,1536,128]{2,1,0:T(8,128)(2,1)S(1)}, bf16[32,1536,128]{2,1,0:T(8,128)(2,1)}, u32[]{:S(2)}) %copy-start.1) | copy-done | bytes 12582936
  85.7 8.0 %sweep.4 = (f32[96,128]{1,0:T(8,128)S(1)}, bf16[96,128]{1,0:T(8,128)(2,1)S(1)}, f32[96,128]{1,0:T(8,128)S(1)}, f32[12,128]{1,0:T(8,128)S(1)}) custom-call(s32[5]{0:T(128)S(1)} %stack.83.at_ref, s32[32,12]{1,0:T(8,128)S(1)} %bitcast.69, s32[2,9,16]{2,1,0:T(8,128)S(1)} %pad_add_fusion.refs_0_, f32[9,16]{1,0:T(8,128)S(1)} %bitcast.81, ...), custom_call_target="tpu_custom_call" | custom-call | tf_op jit(solution)/shard_map/sweep/pallas_call | solution.py:335
  93.7 1.3 collective-permute-start.12
  95.0 4.5 %collective-permute-start.11 = (bf16[96,128]{1,0:T(8,128)(2,1)S(1)}, bf16[96,128]{1,0:T(8,128)(2,1)S(1)}, u32[]{:S(2)}, u32[]{:S(2)}) collective-permute-start(bf16[96,128]{1,0:T(8,128)(2,1)S(1)} %get-tuple-element.24), channel_id=1, source_target_pairs={{0,1},{1,2},{2,3},{3,4},{4,5},{5,6},{6,7},{8,9},{9,10},{10,11},{11... | collective-permute-start | bytes 73736 | tf_op jit(solution)/shard_map/ppermute | solution.py:29
  99.5 1.5 collective-permute-done.11
  101.0 1.3 collective-permute-start.14
  102.3 3.0 %collective-permute-start.13 = (bf16[3,96,128]{2,1,0:T(8,128)(2,1)S(1)}, bf16[3,96,128]{2,1,0:T(8,128)(2,1)S(1)}, u32[]{:S(2)}, u32[]{:S(2)}) collective-permute-start(bf16[3,96,128]{2,1,0:T(8,128)(2,1)S(1)} %pad_maximum_fusion.2.refs_3_), channel_id=1, source_target_pairs={{0,8},{8,16},{16,24},{1,9},{9,17},{17,25},{2,10},{10,18},{18,26},{... | collective-permute-start | bytes 221192 | tf_op jit(solution)/shard_map/ppermute | solution.py:29
  105.4 0.9 collective-permute-done.13.refs_2_
  106.3 5.1 %sweep.5 = (f32[96,128]{1,0:T(8,128)S(1)}, bf16[96,128]{1,0:T(8,128)(2,1)S(1)}) custom-call(s32[5]{0:T(128)S(1)} %stack.83.at_ref, s32[32,12]{1,0:T(8,128)S(1)} %bitcast.70, f32[96,128]{1,0:T(8,128)S(1)} %get-tuple-element.23.refs_0_, f32[3,288,128]{2,1,0:T(8,128)S(1)} %get-tuple-element.21.refs_3_.refs_1_.refs_2_, ...), custom_call_target="tpu_custom_call" | custom-call | tf_op jit(solution)/shard_map/sweep/pallas_call | solution.py:335
  111.4 1.3 collective-permute-start.16
  112.7 5.2 %collective-permute-start.15 = (bf16[96,128]{1,0:T(8,128)(2,1)S(1)}, bf16[96,128]{1,0:T(8,128)(2,1)S(1)}, u32[]{:S(2)}, u32[]{:S(2)}) collective-permute-start(bf16[96,128]{1,0:T(8,128)(2,1)S(1)} %get-tuple-element.27), channel_id=1, source_target_pairs={{0,1},{1,2},{2,3},{3,4},{4,5},{5,6},{6,7},{8,9},{9,10},{10,11},{11... | collective-permute-start | bytes 73736 | tf_op jit(solution)/shard_map/ppermute | solution.py:29
  117.9 1.5 collective-permute-done.15
  119.4 1.3 collective-permute-start.18
  120.7 3.3 %collective-permute-start.17 = (bf16[3,96,128]{2,1,0:T(8,128)(2,1)S(1)}, bf16[3,96,128]{2,1,0:T(8,128)(2,1)S(1)}, u32[]{:S(2)}, u32[]{:S(2)}) collective-permute-start(bf16[3,96,128]{2,1,0:T(8,128)(2,1)S(1)} %pad_maximum_fusion.3.refs_3_), channel_id=1, source_target_pairs={{0,8},{8,16},{16,24},{1,9},{9,17},{17,25},{2,10},{10,18},{18,26},{... | collective-permute-start | bytes 221192 | tf_op jit(solution)/shard_map/ppermute | solution.py:29
  124.0 0.9 collective-permute-done.17.refs_2_
  124.9 5.1 %sweep.6 = (f32[96,128]{1,0:T(8,128)S(1)}, bf16[96,128]{1,0:T(8,128)(2,1)S(1)}) custom-call(s32[5]{0:T(128)S(1)} %stack.83.at_ref, s32[32,12]{1,0:T(8,128)S(1)} %bitcast.71, f32[96,128]{1,0:T(8,128)S(1)} %get-tuple-element.26.refs_0_, f32[3,288,128]{2,1,0:T(8,128)S(1)} %get-tuple-element.21.refs_3_.refs_1_.refs_2_, ...), custom_call_target="tpu_custom_call" | custom-call | tf_op jit(solution)/shard_map/sweep/pallas_call | solution.py:335
  130.0 1.3 collective-permute-start.20
  131.3 5.7 %collective-permute-start.19 = (bf16[96,128]{1,0:T(8,128)(2,1)S(1)}, bf16[96,128]{1,0:T(8,128)(2,1)S(1)}, u32[]{:S(2)}, u32[]{:S(2)}) collective-permute-start(bf16[96,128]{1,0:T(8,128)(2,1)S(1)} %get-tuple-element.29), channel_id=1, source_target_pairs={{0,1},{1,2},{2,3},{3,4},{4,5},{5,6},{6,7},{8,9},{9,10},{10,11},{11... | collective-permute-start | bytes 73736 | tf_op jit(solution)/shard_map/ppermute | solution.py:29
  137.1 1.5 collective-permute-done.19
  138.6 1.3 collective-permute-start.22
  139.9 5.4 %collective-permute-start.21 = (bf16[3,96,128]{2,1,0:T(8,128)(2,1)S(1)}, bf16[3,96,128]{2,1,0:T(8,128)(2,1)S(1)}, u32[]{:S(2)}, u32[]{:S(2)}) collective-permute-start(bf16[3,96,128]{2,1,0:T(8,128)(2,1)S(1)} %pad_maximum_fusion.4.refs_4_), channel_id=1, source_target_pairs={{0,8},{8,16},{16,24},{1,9},{9,17},{17,25},{2,10},{10,18},{18,26},{... | collective-permute-start | bytes 221192 | tf_op jit(solution)/shard_map/ppermute | solution.py:29
  145.3 0.9 collective-permute-done.21.refs_3_
  146.2 6.0 %sweep.7 = (f32[96,128]{1,0:T(8,128)}, f32[32,16,128]{2,1,0:T(8,128)}) custom-call(s32[5]{0:T(128)S(1)} %stack.83.at_ref, s32[32,12]{1,0:T(8,128)S(1)} %bitcast.72, f32[96,128]{1,0:T(8,128)S(1)} %get-tuple-element.28.refs_0_, s32[16]{0:T(128)S(1)} %bitcast.86, f32[3,288,128]{2,1,0:T(8,128)S(1)} %get-tuple-element.21.refs_3_.refs_1_.refs_2_, ...), custom_call_target="tpu_custom_call" | custom-call | tf_op jit(solution)/shard_map/sweep/pallas_call | solution.py:335
  152.3 13.6 %all-to-all-start.1 = ((f32[32,16,128]{2,1,0:T(8,128)}), f32[32,16,128]{2,1,0:T(8,128)S(1)}, u32[]{:S(2)}, u32[]{:S(2)}) async-start(f32[32,16,128]{2,1,0:T(8,128)} %get-tuple-element.34), calls=%async_computation.1 | async-start | bytes 524288 | tf_op jit(solution)/shard_map/all_to_all | solution.py:578
  166.6 9.8 %all-to-all-done.1 = f32[32,16,128]{2,1,0:T(8,128)S(1)} async-done(((f32[32,16,128]{2,1,0:T(8,128)}), f32[32,16,128]{2,1,0:T(8,128)S(1)}, u32[]{:S(2)}, u32[]{:S(2)}) %all-to-all-start.1) | async-done | bytes 262176 | tf_op jit(solution)/shard_map/all_to_all | solution.py:578
  177.0 12.7 %fock_term.1 = f32[3072,1536]{1,0:T(8,128)} custom-call(s32[5]{0:T(128)} %copy-done.14, bf16[3072,256]{1,0:T(8,128)(2,1)} %copy-done.6, bf16[3072,256]{1,0:T(8,128)(2,1)} %copy-done.7, bf16[512,1536]{1,0:T(8,128)(2,1)} %refs_2_.1, f32[3,1536]{1,0:T(4,128)} %refs_3_.1, f32[512,128]{1,0:T(8,128)} %bitcast.87), custom_call_target="tpu_custom_call" | custom-call | tf_op jit(solution)/shard_map/fock_term/pallas_call | solution.py:470
  (65 shorter events, 7.2 us)
Async XLA Ops:
  0.6 12.4 %collective-permute-start.6 = (bf16[64,3072]{1,0:T(8,128)(2,1)}, bf16[64,3072]{1,0:T(8,128)(2,1)S(1)}, u32[]{:S(2)}, u32[]{:S(2)}) collective-permute-start(bf16[64,3072]{1,0:T(8,128)(2,1)} %refs_0_.1), channel_id=1, source_target_pairs={{0,2},{2,4},{4,6},{6,7},{7,5},{5,3},{3,1},{1,0},{8,10},{10,12},{12... | collective-permute-start | bytes 1179656 | tf_op jit(solution)/shard_map/ppermute | solution.py:507
  3.7 18.7 %collective-permute-start.4 = (bf16[64,3072]{1,0:T(8,128)(2,1)}, bf16[64,3072]{1,0:T(8,128)(2,1)S(1)}, u32[]{:S(2)}, u32[]{:S(2)}) collective-permute-start(bf16[64,3072]{1,0:T(8,128)(2,1)} %refs_0_.1), channel_id=1, source_target_pairs={{2,0},{4,2},{6,4},{7,6},{5,7},{3,5},{1,3},{0,1},{10,8},{12,10},{14... | collective-permute-start | bytes 1179656 | tf_op jit(solution)/shard_map/ppermute | solution.py:511
  13.0 11.4 %collective-permute-start.7 = (bf16[64,3072]{1,0:T(8,128)(2,1)S(1)}, bf16[64,3072]{1,0:T(8,128)(2,1)S(1)}, u32[]{:S(2)}, u32[]{:S(2)}) collective-permute-start(bf16[64,3072]{1,0:T(8,128)(2,1)S(1)} %collective-permute-done.6.refs_1_), channel_id=1, source_target_pairs={{0,2},{2,4},{4,6},{6,7},{7,5},{5,3},{3,1},{1,0},{8,10},{10,12},{12... | collective-permute-start | bytes 1179656 | tf_op jit(solution)/shard_map/ppermute | solution.py:507
  16.6 10.0 %collective-permute-start.1 = (f32[200,128]{1,0:T(8,128)S(1)}, f32[200,128]{1,0:T(8,128)S(1)}, u32[]{:S(2)}, u32[]{:S(2)}) collective-permute-start(f32[200,128]{1,0:T(8,128)S(1)} %get-tuple-element.45), channel_id=1, source_target_pairs={{1,0},{2,1},{3,2},{4,3},{5,4},{6,5},{7,6},{9,8},{10,9},{11,10},{12... | collective-permute-start | bytes 307208 | tf_op jit(solution)/shard_map/ppermute | solution.py:29
  17.9 8.7 %collective-permute-start = (f32[200,128]{1,0:T(8,128)S(1)}, f32[200,128]{1,0:T(8,128)S(1)}, u32[]{:S(2)}, u32[]{:S(2)}) collective-permute-start(f32[200,128]{1,0:T(8,128)S(1)} %get-tuple-element.45), channel_id=1, source_target_pairs={{0,1},{1,2},{2,3},{3,4},{4,5},{5,6},{6,7},{8,9},{9,10},{10,11},{11... | collective-permute-start | bytes 307208 | tf_op jit(solution)/shard_map/ppermute | solution.py:29
  22.4 10.0 %collective-permute-start.5 = (bf16[64,3072]{1,0:T(8,128)(2,1)S(1)}, bf16[64,3072]{1,0:T(8,128)(2,1)}, u32[]{:S(2)}, u32[]{:S(2)}) collective-permute-start(bf16[64,3072]{1,0:T(8,128)(2,1)S(1)} %collective-permute-done.4.refs_2_), channel_id=1, source_target_pairs={{2,0},{4,2},{6,4},{7,6},{5,7},{3,5},{1,3},{0,1},{10,8},{12,10},{14... | collective-permute-start | bytes 1179656 | tf_op jit(solution)/shard_map/ppermute | solution.py:511
  24.4 10.6 %copy-start.10 = (bf16[64,3072]{1,0:T(8,128)(2,1)}, bf16[64,3072]{1,0:T(8,128)(2,1)S(1)}, u32[]{:S(2)}) copy-start(bf16[64,3072]{1,0:T(8,128)(2,1)S(1)} %collective-permute-done.7.refs_3_) | copy-start | bytes 1179652
  24.4 10.6 %collective-permute-start.8 = (bf16[64,3072]{1,0:T(8,128)(2,1)S(1)}, bf16[64,3072]{1,0:T(8,128)(2,1)}, u32[]{:S(2)}, u32[]{:S(2)}) collective-permute-start(bf16[64,3072]{1,0:T(8,128)(2,1)S(1)} %collective-permute-done.7.refs_3_), channel_id=1, source_target_pairs={{0,2},{2,4},{4,6},{6,7},{7,5},{5,3},{3,1},{1,0},{8,10},{10,12},{12... | collective-permute-start | bytes 1179656 | tf_op jit(solution)/shard_map/ppermute | solution.py:507
  26.6 8.4 %collective-permute-start.3 = (f32[3,200,128]{2,1,0:T(8,128)S(1)}, f32[3,200,128]{2,1,0:T(8,128)S(1)}, u32[]{:S(2)}, u32[]{:S(2)}) collective-permute-start(f32[3,200,128]{2,1,0:T(8,128)S(1)} %pad_maximum_fusion.mid_ref.refs_5_), channel_id=1, source_target_pairs={{8,0},{16,8},{24,16},{9,1},{17,9},{25,17},{10,2},{18,10},{26,18},{... | collective-permute-start | bytes 921608 | tf_op jit(solution)/shard_map/ppermute | solution.py:29
  28.8 117.4 %copy-start.14 = (s32[5]{0:T(128)}, s32[5]{0:T(128)S(1)}, u32[]{:S(2)}) copy-start(s32[5]{0:T(128)S(1)} %stack.83.at_ref) | copy-start | bytes 64
  28.8 6.2 %collective-permute-start.2 = (f32[3,200,128]{2,1,0:T(8,128)S(1)}, f32[3,200,128]{2,1,0:T(8,128)S(1)}, u32[]{:S(2)}, u32[]{:S(2)}) collective-permute-start(f32[3,200,128]{2,1,0:T(8,128)S(1)} %pad_maximum_fusion.mid_ref.refs_5_), channel_id=1, source_target_pairs={{0,8},{8,16},{16,24},{1,9},{9,17},{17,25},{2,10},{10,18},{18,26},{... | collective-permute-start | bytes 921608 | tf_op jit(solution)/shard_map/ppermute | solution.py:29
  32.4 17.7 %collective-permute-start.9 = (bf16[64,3072]{1,0:T(8,128)(2,1)}, bf16[64,3072]{1,0:T(8,128)(2,1)S(1)}, u32[]{:S(2)}, u32[]{:S(2)}) collective-permute-start(bf16[64,3072]{1,0:T(8,128)(2,1)} %collective-permute-done.5.refs_0_), channel_id=1, source_target_pairs={{2,0},{4,2},{6,4},{7,6},{5,7},{3,5},{1,3},{0,1},{10,8},{12,10},{14... | collective-permute-start | bytes 1179656 | tf_op jit(solution)/shard_map/ppermute | solution.py:511
  35.0 15.1 %collective-permute-start.10 = (bf16[64,3072]{1,0:T(8,128)(2,1)}, bf16[64,3072]{1,0:T(8,128)(2,1)S(1)}, u32[]{:S(2)}, u32[]{:S(2)}) collective-permute-start(bf16[64,3072]{1,0:T(8,128)(2,1)} %collective-permute-done.8.refs_1_), channel_id=1, source_target_pairs={{0,2},{2,4},{4,6},{6,7},{7,5},{5,3},{3,1},{1,0},{8,10},{10,12},{12... | collective-permute-start | bytes 1179656 | tf_op jit(solution)/shard_map/ppermute | solution.py:507
  35.0 1.4 copy-start.3
  36.5 3.7 %copy-start.5 = (bf16[3072,1536]{1,0:T(8,128)(2,1)S(1)}, bf16[3072,1536]{1,0:T(8,128)(2,1)}, u32[]{:S(2)}) copy-start(bf16[3072,1536]{1,0:T(8,128)(2,1)} %refs_4_.3) | copy-start | bytes 28311556
  40.1 1.0 copy-start.9
  41.1 1.0 copy-start.11
  42.1 0.7 copy-start.12
  42.9 7.2 %copy-start.4 = (bf16[512,1536]{1,0:T(8,128)(2,1)S(1)}, bf16[512,1536]{1,0:T(8,128)(2,1)}, u32[]{:S(2)}) copy-start(bf16[512,1536]{1,0:T(8,128)(2,1)} %refs_2_.1) | copy-start | bytes 4718596
  48.9 1.2 copy-start.6
  50.1 31.0 %copy-start.8 = (f32[1,1,4096]{2,1,0:T(1,128)S(1)}, f32[1,1,4096]{2,1,0:T(1,128)}, u32[]{:S(2)}) copy-start(f32[1,1,4096]{2,1,0:T(1,128)} %param.14) | copy-start | bytes 49156
  50.1 31.0 %copy-start.13 = (f32[3,1,1,4096]{3,2,1,0:T(1,128)S(1)}, f32[3,1,1,4096]{3,2,1,0:T(1,128)}, u32[]{:S(2)}) copy-start(f32[3,1,1,4096]{3,2,1,0:T(1,128)} %param.15) | copy-start | bytes 147460
  57.8 1.1 copy-start.7
  59.0 22.1 %all-to-all-start = ((f32[32,12,128]{2,1,0:T(8,128)}), f32[32,12,128]{2,1,0:T(8,128)S(1)}, u32[]{:S(2)}, u32[]{:S(2)}) async-start(f32[32,12,128]{2,1,0:T(8,128)} %get-tuple-element.20), calls=%async_computation | async-start | bytes 524288 | tf_op jit(solution)/shard_map/all_to_all | solution.py:554
  76.3 4.8 %copy-start = (bf16[32,1536,128]{2,1,0:T(8,128)(2,1)}, bf16[32,1536,128]{2,1,0:T(8,128)(2,1)S(1)}, u32[]{:S(2)}) copy-start(bf16[32,1536,128]{2,1,0:T(8,128)(2,1)S(1)} %get-tuple-element.22.refs_7_.refs_5_.refs_6_) | copy-start | bytes 37748740
  81.1 4.6 %copy-start.1 = (bf16[32,1536,128]{2,1,0:T(8,128)(2,1)S(1)}, bf16[32,1536,128]{2,1,0:T(8,128)(2,1)}, u32[]{:S(2)}) copy-start(bf16[32,1536,128]{2,1,0:T(8,128)(2,1)} %copy-done) | copy-start | bytes 37748740
  85.7 20.6 %copy-start.2 = (bf16[32,1536,128]{2,1,0:T(8,128)(2,1)S(1)}, bf16[32,1536,128]{2,1,0:T(8,128)(2,1)}, u32[]{:S(2)}) copy-start(bf16[32,1536,128]{2,1,0:T(8,128)(2,1)} %copy-done) | copy-start | bytes 37748740
  93.7 5.9 %collective-permute-start.12 = (bf16[96,128]{1,0:T(8,128)(2,1)S(1)}, bf16[96,128]{1,0:T(8,128)(2,1)S(1)}, u32[]{:S(2)}, u32[]{:S(2)}) collective-permute-start(bf16[96,128]{1,0:T(8,128)(2,1)S(1)} %get-tuple-element.24), channel_id=1, source_target_pairs={{1,0},{2,1},{3,2},{4,3},{5,4},{6,5},{7,6},{9,8},{10,9},{11,10},{12... | collective-permute-start | bytes 73736 | tf_op jit(solution)/shard_map/ppermute | solution.py:29
  95.0 6.1 %collective-permute-start.11 = (bf16[96,128]{1,0:T(8,128)(2,1)S(1)}, bf16[96,128]{1,0:T(8,128)(2,1)S(1)}, u32[]{:S(2)}, u32[]{:S(2)}) collective-permute-start(bf16[96,128]{1,0:T(8,128)(2,1)S(1)} %get-tuple-element.24), channel_id=1, source_target_pairs={{0,1},{1,2},{2,3},{3,4},{4,5},{5,6},{6,7},{8,9},{9,10},{10,11},{11... | collective-permute-start | bytes 73736 | tf_op jit(solution)/shard_map/ppermute | solution.py:29
  101.0 4.3 %collective-permute-start.14 = (bf16[3,96,128]{2,1,0:T(8,128)(2,1)S(1)}, bf16[3,96,128]{2,1,0:T(8,128)(2,1)S(1)}, u32[]{:S(2)}, u32[]{:S(2)}) collective-permute-start(bf16[3,96,128]{2,1,0:T(8,128)(2,1)S(1)} %pad_maximum_fusion.2.refs_3_), channel_id=1, source_target_pairs={{8,0},{16,8},{24,16},{9,1},{17,9},{25,17},{10,2},{18,10},{26,18},{... | collective-permute-start | bytes 221192 | tf_op jit(solution)/shard_map/ppermute | solution.py:29
  102.3 3.9 %collective-permute-start.13 = (bf16[3,96,128]{2,1,0:T(8,128)(2,1)S(1)}, bf16[3,96,128]{2,1,0:T(8,128)(2,1)S(1)}, u32[]{:S(2)}, u32[]{:S(2)}) collective-permute-start(bf16[3,96,128]{2,1,0:T(8,128)(2,1)S(1)} %pad_maximum_fusion.2.refs_3_), channel_id=1, source_target_pairs={{0,8},{8,16},{16,24},{1,9},{9,17},{17,25},{2,10},{10,18},{18,26},{... | collective-permute-start | bytes 221192 | tf_op jit(solution)/shard_map/ppermute | solution.py:29
  111.4 34.8 %copy-start.15 = (s32[1,1,16]{2,1,0:T(1,128)S(1)}, s32[1,1,16]{2,1,0:T(1,128)}, u32[]{:S(2)}) copy-start(s32[1,1,16]{2,1,0:T(1,128)} %param.17) | copy-start | bytes 196
  111.4 6.5 %collective-permute-start.16 = (bf16[96,128]{1,0:T(8,128)(2,1)S(1)}, bf16[96,128]{1,0:T(8,128)(2,1)S(1)}, u32[]{:S(2)}, u32[]{:S(2)}) collective-permute-start(bf16[96,128]{1,0:T(8,128)(2,1)S(1)} %get-tuple-element.27), channel_id=1, source_target_pairs={{1,0},{2,1},{3,2},{4,3},{5,4},{6,5},{7,6},{9,8},{10,9},{11,10},{12... | collective-permute-start | bytes 73736 | tf_op jit(solution)/shard_map/ppermute | solution.py:29
  112.7 6.7 %collective-permute-start.15 = (bf16[96,128]{1,0:T(8,128)(2,1)S(1)}, bf16[96,128]{1,0:T(8,128)(2,1)S(1)}, u32[]{:S(2)}, u32[]{:S(2)}) collective-permute-start(bf16[96,128]{1,0:T(8,128)(2,1)S(1)} %get-tuple-element.27), channel_id=1, source_target_pairs={{0,1},{1,2},{2,3},{3,4},{4,5},{5,6},{6,7},{8,9},{9,10},{10,11},{11... | collective-permute-start | bytes 73736 | tf_op jit(solution)/shard_map/ppermute | solution.py:29
  119.4 4.6 %collective-permute-start.18 = (bf16[3,96,128]{2,1,0:T(8,128)(2,1)S(1)}, bf16[3,96,128]{2,1,0:T(8,128)(2,1)S(1)}, u32[]{:S(2)}, u32[]{:S(2)}) collective-permute-start(bf16[3,96,128]{2,1,0:T(8,128)(2,1)S(1)} %pad_maximum_fusion.3.refs_3_), channel_id=1, source_target_pairs={{8,0},{16,8},{24,16},{9,1},{17,9},{25,17},{10,2},{18,10},{26,18},{... | collective-permute-start | bytes 221192 | tf_op jit(solution)/shard_map/ppermute | solution.py:29
  120.7 4.2 %collective-permute-start.17 = (bf16[3,96,128]{2,1,0:T(8,128)(2,1)S(1)}, bf16[3,96,128]{2,1,0:T(8,128)(2,1)S(1)}, u32[]{:S(2)}, u32[]{:S(2)}) collective-permute-start(bf16[3,96,128]{2,1,0:T(8,128)(2,1)S(1)} %pad_maximum_fusion.3.refs_3_), channel_id=1, source_target_pairs={{0,8},{8,16},{16,24},{1,9},{9,17},{17,25},{2,10},{10,18},{18,26},{... | collective-permute-start | bytes 221192 | tf_op jit(solution)/shard_map/ppermute | solution.py:29
  130.0 7.0 %collective-permute-start.20 = (bf16[96,128]{1,0:T(8,128)(2,1)S(1)}, bf16[96,128]{1,0:T(8,128)(2,1)S(1)}, u32[]{:S(2)}, u32[]{:S(2)}) collective-permute-start(bf16[96,128]{1,0:T(8,128)(2,1)S(1)} %get-tuple-element.29), channel_id=1, source_target_pairs={{1,0},{2,1},{3,2},{4,3},{5,4},{6,5},{7,6},{9,8},{10,9},{11,10},{12... | collective-permute-start | bytes 73736 | tf_op jit(solution)/shard_map/ppermute | solution.py:29
  131.3 7.2 %collective-permute-start.19 = (bf16[96,128]{1,0:T(8,128)(2,1)S(1)}, bf16[96,128]{1,0:T(8,128)(2,1)S(1)}, u32[]{:S(2)}, u32[]{:S(2)}) collective-permute-start(bf16[96,128]{1,0:T(8,128)(2,1)S(1)} %get-tuple-element.29), channel_id=1, source_target_pairs={{0,1},{1,2},{2,3},{3,4},{4,5},{5,6},{6,7},{8,9},{9,10},{10,11},{11... | collective-permute-start | bytes 73736 | tf_op jit(solution)/shard_map/ppermute | solution.py:29
  138.6 6.7 %collective-permute-start.22 = (bf16[3,96,128]{2,1,0:T(8,128)(2,1)S(1)}, bf16[3,96,128]{2,1,0:T(8,128)(2,1)S(1)}, u32[]{:S(2)}, u32[]{:S(2)}) collective-permute-start(bf16[3,96,128]{2,1,0:T(8,128)(2,1)S(1)} %pad_maximum_fusion.4.refs_4_), channel_id=1, source_target_pairs={{8,0},{16,8},{24,16},{9,1},{17,9},{25,17},{10,2},{18,10},{26,18},{... | collective-permute-start | bytes 221192 | tf_op jit(solution)/shard_map/ppermute | solution.py:29
  139.9 6.3 %collective-permute-start.21 = (bf16[3,96,128]{2,1,0:T(8,128)(2,1)S(1)}, bf16[3,96,128]{2,1,0:T(8,128)(2,1)S(1)}, u32[]{:S(2)}, u32[]{:S(2)}) collective-permute-start(bf16[3,96,128]{2,1,0:T(8,128)(2,1)S(1)} %pad_maximum_fusion.4.refs_4_), channel_id=1, source_target_pairs={{0,8},{8,16},{16,24},{1,9},{9,17},{17,25},{2,10},{10,18},{18,26},{... | collective-permute-start | bytes 221192 | tf_op jit(solution)/shard_map/ppermute | solution.py:29
  152.3 24.1 %all-to-all-start.1 = ((f32[32,16,128]{2,1,0:T(8,128)}), f32[32,16,128]{2,1,0:T(8,128)S(1)}, u32[]{:S(2)}, u32[]{:S(2)}) async-start(f32[32,16,128]{2,1,0:T(8,128)} %get-tuple-element.34), calls=%async_computation.1 | async-start | bytes 524288 | tf_op jit(solution)/shard_map/all_to_all | solution.py:578
  176.3 0.7 copy-start.16
